TPU v7x, 32 devices: a 4x4x1 block of a 4x4x8 slice. The times are simulated.
32 devices in a mesh: rep: 1 (over z), kv: 32 (over y, x, core).
Axes of the slice: x: 4, y: 4, z: 1, core: 2. Of those that a mesh axis runs over, the one named last changes fastest.
The devices are a block of a 4x4x8 slice.
Arguments:
- embeds: bfloat16 [2, 2048, 2048], P(None, ('rep', 'kv'))
- w_query: bfloat16 [2, 2048, 2048], replicated
- w_key: bfloat16 [2, 2048, 256], replicated
- w_value: bfloat16 [2, 2048, 256], replicated
- w_out: bfloat16 [2, 2048, 2048], replicated
- w_up: bfloat16 [2, 2048, 11008], replicated
- w_down: bfloat16 [2, 11008, 2048], replicated
- k_pool: bfloat16 [6144, 2, 32, 2, 128], P(('rep', 'kv'))
- v_pool: bfloat16 [6144, 2, 32, 2, 128], P(('rep', 'kv'))
- new_table: int32 [2048, 2], P('rep')
- seq_lens: int32 [2048], P('rep')
- mig_src: int32 [64], P('rep')
- mig_dst: int32 [64], P('rep')
Outputs:
- output 1: bfloat16 [2, 2048, 2048], P(None, ('rep', 'kv'))
- output 2: bfloat16 [6144, 2, 32, 2, 128], P(('rep', 'kv'))
- output 3: bfloat16 [6144, 2, 32, 2, 128], P(('rep', 'kv'))
All inputs are finite; a program needn't handle non-finite values.
Results may differ from a plain program's by a relative error of at most 0.0164352.
Values are sent between devices in bfloat16 or wider.
A program may use at most 768 MiB of HBM per device.

v0:
```python
import functools
import math

import jax
import jax.numpy as jnp
from jax import lax
from jax.experimental import pallas as pl
from jax.experimental.pallas import tpu as pltpu
from jax.sharding import PartitionSpec as P

ANY = pl.BlockSpec(memory_space=pl.ANY)
SMEM = pl.BlockSpec(memory_space=pltpu.SMEM)
VMEM = pl.BlockSpec(memory_space=pltpu.VMEM)
DMA = pltpu.SemaphoreType.DMA
CHUNK = 256
UNROLL = 8
LIMIT = 63 << 20
F32, BF16 = jnp.float32, jnp.bfloat16


def aligned(x, multiple):
    return x if isinstance(x, int) else pl.multiple_of(x, multiple)


class Dims:
    def __init__(self, rows, weights, k_pool, page):
        w_query, w_key, _, _, w_up, _ = weights
        self.layers, self.width, self.q_width = w_query.shape
        self.ff = w_up.shape[2]
        self.slots, _, self.page_rows, self.head_dim = k_pool.shape
        self.kv_heads = w_key.shape[2] // self.head_dim
        self.heads = self.q_width // self.head_dim
        self.page, self.rows = page, rows
        self.tokens = 2 * rows
        self.stride = self.tokens + 8
        self.n_q, self.n_o, self.n_u = self.q_width // CHUNK, self.width // CHUNK, self.ff // CHUNK
        self.col_layer = self.n_q + 2 + self.n_o + self.n_u

    def compute_scratch(self, n_col, n_row):
        return [
            pltpu.VMEM((n_col, self.width, CHUNK), BF16),
            pltpu.VMEM((n_row, CHUNK, self.width), BF16),
            pltpu.VMEM((self.heads * self.stride, self.head_dim), F32),
            pltpu.VMEM((self.kv_heads * self.stride, self.head_dim), F32),
            pltpu.VMEM((self.kv_heads * self.stride, self.head_dim), F32),
            pltpu.VMEM((self.heads * self.stride, self.head_dim), F32),
            pltpu.VMEM((self.tokens, self.q_width), BF16),
            pltpu.VMEM((self.tokens, self.ff), BF16),
            pltpu.VMEM((self.tokens, self.width), F32),
            DMA((n_col,)),
            DMA((n_row,)),
        ]

    def cost(self, layers):
        size = layers * self.width * (2 * self.q_width + 2 * self.kv_heads * self.head_dim + 2 * self.ff)
        return pl.CostEstimate(flops=2 * size * self.tokens, bytes_accessed=2 * size, transcendentals=0)


class Decoder:
    def __init__(self, dims, first, layers, weights, y_ref, scratch, group=2, unroll=UNROLL):
        self.group, self.unroll = group, unroll
        self.d, self.first, self.layers, self.weights, self.y_ref = dims, first, layers, weights, y_ref
        (self.col_buf, self.row_buf, self.q_s, self.kn_s, self.vn_s, self.o_s, self.att, self.act, self.acc, self.col_sem, self.row_sem) = scratch
        self.n_col, self.n_row = self.col_buf.shape[0], self.row_buf.shape[0]
        self.zero = lax.axis_index('kv') * 0
        d = dims
        cols = 2 * d.page * d.kv_heads
        col_pos = lax.broadcasted_iota(jnp.int32, (2 * d.heads, cols), 1)
        row_pos = lax.broadcasted_iota(jnp.int32, (2 * d.heads, cols), 0)
        same_head = (col_pos % d.kv_heads) == (row_pos % d.heads) // (d.heads // d.kv_heads)
        self.limit = jnp.where(same_head, col_pos // d.kv_heads - row_pos // d.heads, 4 * d.page)
        self.page_pos = lax.broadcasted_iota(jnp.int32, (d.page_rows, d.head_dim), 0) // d.kv_heads
        self.tile_head = lax.broadcasted_iota(jnp.int32, (8, d.head_dim), 0) % d.kv_heads

    def layer_of(self, g, per_layer):
        return sum((g >= per_layer * l).astype(jnp.int32) for l in range(1, self.layers))

    def col_start(self, g):
        d = self.d
        wq, wk, wv, wo, wu, _ = self.weights

        @pl.when(g < self.layers * d.col_layer)
        def _():
            layer = self.layer_of(g, d.col_layer)
            pos = g - layer * d.col_layer
            slot = g % self.n_col

            def go(src, c):
                start = aligned(c * CHUNK, CHUNK)
                pltpu.make_async_copy(src.at[self.first + layer].at[:, pl.ds(start, CHUNK)], self.col_buf.at[slot], self.col_sem.at[slot]).start()

            @pl.when(pos < d.n_q)
            def _():
                go(wq, pos)

            @pl.when(pos == d.n_q)
            def _():
                go(wk, 0)

            @pl.when(pos == d.n_q + 1)
            def _():
                go(wv, 0)

            @pl.when((pos >= d.n_q + 2) & (pos < d.n_q + 2 + d.n_o))
            def _():
                go(wo, pos - (d.n_q + 2))

            @pl.when(pos >= d.n_q + 2 + d.n_o)
            def _():
                go(wu, pos - (d.n_q + 2 + d.n_o))

    def row_start(self, g):
        d = self.d
        wd = self.weights[5]

        @pl.when(g < self.layers * d.n_u)
        def _():
            layer = self.layer_of(g, d.n_u)
            slot = g % self.n_row
            start = aligned((g - layer * d.n_u) * CHUNK, CHUNK)
            pltpu.make_async_copy(wd.at[self.first + layer].at[pl.ds(start, CHUNK)], self.row_buf.at[slot], self.row_sem.at[slot]).start()

    def start_stream(self):
        @pl.loop(0, self.n_col)
        def _(g):
            self.col_start(g)

        @pl.loop(0, self.n_row)
        def _(g):
            self.row_start(g)

    def with_cols(self, g, count, body):
        slots = [(g + u) % self.n_col for u in range(count)]
        for slot in slots:
            pltpu.make_async_copy(self.weights[1].at[0], self.col_buf.at[slot], self.col_sem.at[slot]).wait()
        body([self.col_buf.at[slot] for slot in slots])
        for u in range(count):
            self.col_start(g + u + self.n_col)

    def with_rows(self, g, count, body):
        slots = [(g + u) % self.n_row for u in range(count)]
        for slot in slots:
            pltpu.make_async_copy(self.weights[5].at[0, pl.ds(0, CHUNK), :], self.row_buf.at[slot], self.row_sem.at[slot]).wait()
        body([self.row_buf.at[slot] for slot in slots])
        for u in range(count):
            self.row_start(g + u + self.n_row)

    def project(self, layer):
        d = self.d
        col0 = (self.zero + layer) * d.col_layer

        def product(ref):
            return jnp.dot(self.y_ref[...], ref[...], preferred_element_type=F32).astype(BF16).astype(F32)

        def put(dst, first, out):
            for h in range(CHUNK // d.head_dim):
                at = aligned((first + h) * d.stride, 8)
                dst[pl.ds(at, d.tokens), :] = out[:, h * d.head_dim:(h + 1) * d.head_dim]

        many = self.group

        @pl.loop(0, d.n_q // many)
        def _(j):
            def body(refs):
                outs = [product(ref) for ref in refs]
                for u in range(many):
                    put(self.q_s, (many * j + u) * (CHUNK // d.head_dim), outs[u])

            self.with_cols(col0 + many * j, many, body)

        def body(refs):
            outs = [product(ref) for ref in refs]
            put(self.kn_s, 0, outs[0])
            put(self.vn_s, 0, outs[1])

        self.with_cols(col0 + d.n_q, 2, body)

    def insert(self, page, n, row):
        d = self.d
        val = page.astype(F32)
        for t in range(2):
            new = jnp.broadcast_to(row(t, 0), (8, d.head_dim))
            for g in range(1, d.kv_heads):
                new = jnp.where(self.tile_head == g, row(t, g), new)
            val = jnp.where(self.page_pos == n - d.page + t, jnp.concatenate([new] * (d.page_rows // 8), axis=0), val)
        return val.astype(BF16)

    def attend(self, lens, first_page, last_page, put_page, events=(), begin=0, count=None):
        d = self.d
        count = count or d.rows
        unroll = min(self.unroll, count)

        def some(first):
            ids = [first + u for u in range(unroll)]
            scores, vals = [], []
            for i in ids:
                n = lens(i)

                def updated(p, new_ref):
                    val = self.insert(last_page(p, i), n, lambda t, g: new_ref[pl.ds(g * d.stride + t * d.rows + i, 1), :])
                    put_page(p, i, val)
                    return val

                keys = jnp.concatenate([first_page(0, i), updated(0, self.kn_s)], axis=0)
                vals.append(updated(1, self.vn_s))
                qs = jnp.concatenate([self.q_s[pl.ds(t * d.rows + i, d.heads, stride=d.stride), :] for t in range(2)], axis=0)
                score = lax.dot_general(qs.astype(BF16), keys, (((1,), (1,)), ((), ())), preferred_element_type=F32) * d.head_dim ** -0.5
                scores.append(jnp.where(self.limit <= n, score, -jnp.inf))
            tops = [jnp.max(score, axis=1, keepdims=True) for score in scores]
            probs = [jnp.exp(score - top) for score, top in zip(scores, tops)]
            totals = [jnp.sum(prob, axis=1, keepdims=True) for prob in probs]
            for u, i in enumerate(ids):
                both = jnp.concatenate([first_page(1, i), vals[u]], axis=0)
                out = jnp.dot(probs[u].astype(BF16), both, preferred_element_type=F32) / totals[u]
                for t in range(2):
                    self.o_s[pl.ds(t * d.rows + i, d.heads, stride=d.stride), :] = out[t * d.heads:(t + 1) * d.heads]

        @pl.loop(0, count // unroll)
        def _(block):
            for k, run in events:
                pl.when(block == k)(run)
            some(begin + block * unroll)

    def gather_heads(self):
        d = self.d
        for h in range(d.heads):
            self.att[:, h * d.head_dim:(h + 1) * d.head_dim] = self.o_s[h * d.stride:h * d.stride + d.tokens, :].astype(BF16)

    def mix(self, layer, events=()):
        d = self.d
        layer = self.zero + layer
        col0 = layer * d.col_layer + d.n_q + 2
        many = self.group
        pairs = d.n_u // many

        def between(j, first):
            for k, run in events:
                if first <= k < first + pairs:
                    pl.when(j == k - first)(run)

        def span(j):
            return pl.ds(aligned(j * CHUNK, CHUNK), CHUNK)

        @pl.loop(0, d.n_o // many)
        def _(j):
            def body(refs):
                outs = [jnp.dot(self.att[...], ref[...], preferred_element_type=F32) for ref in refs]
                for u in range(many):
                    at = span(many * j + u)
                    self.y_ref[:, at] = (self.y_ref[:, at].astype(F32) + outs[u]).astype(BF16)

            self.with_cols(col0 + many * j, many, body)

        def up(first, count):
            def body(refs):
                ups = [jnp.dot(self.y_ref[...], ref[...], preferred_element_type=F32) for ref in refs]
                for u in range(count):
                    self.act[:, span(first + u)] = jax.nn.gelu(ups[u].astype(BF16).astype(F32), approximate=True).astype(BF16)

            self.with_cols(col0 + d.n_o + first, count, body)

        def down(first, count):
            def body(refs):
                out = self.acc[...]
                for u in range(count):
                    out += jnp.dot(self.act[:, span(first + u)], refs[u][...], preferred_element_type=F32)
                self.acc[...] = out

            self.with_rows(layer * d.n_u + first, count, body)

        @pl.loop(0, pairs)
        def _(j):
            between(j, 0)
            up(many * j, many)

        if d.n_u % many:
            up(d.n_u - 1, 1)

        self.acc[...] = self.y_ref[...].astype(F32)

        @pl.loop(0, pairs)
        def _(j):
            between(j, pairs)
            down(many * j, many)

        if d.n_u % many:
            down(d.n_u - 1, 1)

        self.y_ref[...] = self.acc[...].astype(BF16)


class Exchange:
    STEPS = 11

    def __init__(self, side, layer, work, core_buf, ring_buf, out, send_sem, recv_sem):
        self.layer = layer
        self.work, self.core_buf, self.ring_buf, self.out, self.send_sem, self.recv_sem = work, core_buf, ring_buf, out, send_sem, recv_sem
        me = lax.axis_index('kv')
        core, x, y = me % 2, me // 2 % side, me // (2 * side)

        def pairings(pos, stride):
            return (((pos + 1) // 2 % 2, me + (1 - 2 * (pos % 2)) * stride), (pos // 2, me + (side - 1 - 2 * pos) * stride))

        xs, ys = pairings(x, 2), pairings(y, 2 * side)
        self.orders = [xs + ys, xs[::-1] + ys[::-1], ys + xs, ys[::-1] + xs[::-1]]
        self.partner = me + 1 - 2 * core
        self.peers = [self.partner] + [dev for _, dev in xs + ys]
        self.half = work.shape[1] // 2
        self.stream = self.half // 4
        self.base, self.other = core * self.half, (1 - core) * self.half
        self.copies, self.done = [], 0
        self.path = [[self.base + k * self.stream for k in range(4)]]
        self.away = []
        for ring in range(4):
            size = self.stream >> (ring + 1)
            self.away.append([self.path[-1][k] + (1 - self.orders[k][ring][0]) * size for k in range(4)])
            self.path.append([self.path[-1][k] + self.orders[k][ring][0] * size for k in range(4)])

    def send(self, src, dst, step, lane, dev):
        def copy():
            return pltpu.make_async_remote_copy(src(), dst(), self.send_sem.at[self.layer, step, lane], self.recv_sem.at[self.layer, step, lane], device_id={'kv': dev})

        copy().start()
        self.copies.append(copy)

    def units(self, ref, at, count):
        return lambda: ref.at[self.layer].at[pl.ds(at, count)]

    def results(self, at, count):
        return lambda: self.out.at[pl.ds(at, count)]

    def add(self, dst_at, buf, src_at, count):
        @pl.loop(0, count)
        def _(u):
            self.work[self.layer, dst_at + u] = self.work[self.layer, dst_at + u] + buf[self.layer, src_at + u]

    def halve(self, ring, k):
        size = self.stream >> (ring + 1)
        src = self.units(self.work, self.away[ring][k], size)
        self.send(src, self.units(self.ring_buf, (k + 1) * self.stream - 2 * size, size), 1 + ring, k, self.orders[k][ring][1])

    def halved(self, ring, k):
        size = self.stream >> (ring + 1)
        self.add(self.path[ring + 1][k], self.ring_buf, (k + 1) * self.stream - 2 * size, size)

    def double(self, ring, k):
        at = self.results(self.path[ring + 1][k], self.stream >> (ring + 1))
        self.send(at, at, 8 - ring, k, self.orders[k][ring][1])

    def step(self):
        step, self.done = self.done, self.done + 1
        started, self.copies = self.copies, []
        if step in (1, 9, 10):
            for copy in started:
                copy().wait()
        if step == 0:
            self.send(self.units(self.work, self.other, self.half), self.units(self.core_buf, 0, self.half), 0, 0, self.partner)
        elif step == 1:
            self.add(self.base, self.core_buf, 0, self.half)
            for k in range(4):
                self.halve(0, k)
        elif step < 9:
            for k in range(4):
                started[k]().wait()
                if step < 6:
                    self.halved(step - 2, k)
                if step < 5:
                    self.halve(step - 1, k)
                    continue
                if step == 5:
                    for u in range(self.stream >> 4):
                        self.out[self.path[4][k] + u] = self.work[self.layer, self.path[4][k] + u]
                self.double(8 - step, k)
        elif step == 9:
            at = self.results(self.base, self.half)
            self.send(at, at, 9, 0, self.partner)


def adjacent_kernel(dims, side, group_size, entries, src_s, dst_s, table_hbm, lens_hbm, embeds_hbm, wq, wk, wv, wo, wu, wd, k_hbm, v_hbm,
                    ya_ref, yb_ref, info_s, last_out,
                    table_s, lens_s, table_v, embeds_v, y_ref, send_buf, got_buf, last_buf, new_buf, work, core_buf, ring_buf, mid_in, mid_out, x_in, plan_v, plan_s, *rest):
    d = dims
    migs, rest = rest[:d.layers], rest[d.layers:]
    pools, rest = [rest[2 * l:2 * l + 2] for l in range(d.layers)], rest[2 * d.layers:]
    compute, (load_sem, pool_sem, plan_sem, x_send, x_recv, page_send, page_recv, new_send, new_recv, mig_send, mig_recv, out_sem) = rest[:-12], rest[-12:]
    half = d.rows // 2
    me = lax.axis_index('kv')
    ahead, behind = lax.rem(me + 1, group_size), lax.rem(me + group_size - 1, group_size)
    dec = Decoder(d, 0, d.layers, (wq, wk, wv, wo, wu, wd), y_ref, compute)
    exchanges = [Exchange(side, l, work, core_buf, ring_buf, migs[l], mig_send, mig_recv) for l in range(d.layers)]

    def scope(name, run, *args):
        with jax.named_scope(name):
            return run(*args)

    pool_loads = [[pltpu.make_async_copy(src.at[:, l], pools[l][p], pool_sem.at[l, p]) for p, src in enumerate((k_hbm, v_hbm))] for l in range(d.layers)]
    embeds_load, table_load, lens_load, table_load_v = [
        pltpu.make_async_copy(src, dst, load_sem.at[i]) for i, (src, dst) in enumerate(((embeds_hbm, embeds_v), (table_hbm, table_s), (lens_hbm, lens_s), (table_hbm, table_v)))]
    for load in [embeds_load] + pool_loads[0] + [table_load, table_load_v, lens_load]:
        load.start()
    barrier = pltpu.get_barrier_semaphore()

    @pl.loop(1, group_size)
    def _(r):
        pl.semaphore_signal(barrier, inc=1, device_id={'kv': lax.rem(me + r, group_size)})

    scope("barrier", lambda: pl.semaphore_wait(barrier, group_size - 1))

    groups = d.tokens // 8
    splits = group_size // groups
    cols = d.width // splits

    def piece(ref, m):
        return ref.at[m // splits, :, pl.ds(aligned(m % splits * cols, cols), cols)]

    def all_pieces(phase):
        some = mid_in.at[pl.ds(0, group_size - 1)]
        pltpu.make_async_remote_copy(some, some, x_send.at[phase], x_recv.at[phase], device_id={'kv': me}).wait()

    def send_embeddings():
        embeds_load.wait()

        @pl.loop(1, group_size)
        def _(r):
            m = lax.rem(me + r, group_size)
            pltpu.make_async_remote_copy(piece(embeds_v, m), mid_in.at[me], x_send.at[0], x_recv.at[0], device_id={'kv': m}).start()

        mid_in[me] = piece(embeds_v, me)[...]

    def load_tables():
        for load in (table_load, lens_load, table_load_v):
            load.wait()
        return lax.rem(table_s[1, 0] // d.slots + group_size, group_size)

    scope("pool_wait_0", lambda: [load.wait() for load in pool_loads[0]])

    def own(l):
        @pl.loop(0, entries)
        def _(e):
            slot = src_s[e] - me * d.slots
            mine = (slot >= 0) & (slot < d.slots)
            slot = jnp.clip(slot, 0, d.slots - 1)
            for p in range(2):
                page = pools[l][p][slot]
                work[l, p * entries + e] = jnp.where(mine, page, jnp.zeros_like(page))

    def step(l):
        scope(f"exchange_{l}_{exchanges[l].done}", exchanges[l].step)

    step_0, step_1 = functools.partial(step, 0), functools.partial(step, 1)

    scope("own_0", own, 0)
    step_0()
    for l in range(1, d.layers):
        for load in pool_loads[l]:
            load.start()
    scope("start_stream", dec.start_stream)
    shift = scope("load_tables", load_tables)
    home_a = lax.rem(me - shift + group_size, group_size)
    home_b = lax.rem(home_a + 1, group_size)

    def clipped(slot):
        return jnp.clip(slot - me * d.slots, 0, d.slots - 1)

    def first_here(l, p, i):
        return pools[l][p][clipped(table_s[0, home_b * d.rows + i])]

    def last_here(l, p, i):
        return pools[l][p][clipped(table_s[1, home_a * d.rows + i])]

    def migrated(l, p, home, i, page):
        entry = plan_s[0, home * d.rows + i]
        return jnp.where(entry >= 0, migs[l][p * entries + jnp.maximum(entry, 0)], page)

    def pack(l):
        @pl.loop(0, half)
        def _(i):
            for p in range(2):
                send_buf[l, 0, p, i] = first_here(l, p, i)
                send_buf[l, 1, p, i] = last_here(l, p, half + i)

    parts = 4
    size = half // parts

    def page_copy(l, way, p, rows):
        return pltpu.make_async_remote_copy(
            send_buf.at[l, way, p, rows], got_buf.at[l, way, p, rows], page_send.at[l, way, p], page_recv.at[l, way, p], device_id={'kv': (ahead, behind)[way]})

    pieces = [iter([(p, part) for part in range(parts) for p in range(2)]) for _ in range(d.layers)]

    def pages_start(l):
        p, part = next(pieces[l])
        for way in range(2):
            page_copy(l, way, p, pl.ds(part * size, size)).start()

    pages_0, pages_1 = functools.partial(pages_start, 0), functools.partial(pages_start, 1)

    def pages_wait(l):
        for way in range(2):
            for p in range(2):
                page_copy(l, way, p, pl.ds(0, half)).wait()

    def pass_on():
        all_pieces(0)
        later = me // splits * 8 % d.rows // half

        @pl.loop(0, group_size)
        def _(m):
            mid_out[m] = mid_in[lax.rem(m - shift + later + group_size, group_size)]

        @pl.loop(1, group_size)
        def _(r):
            m = lax.rem(me + r, group_size)
            pltpu.make_async_remote_copy(mid_out.at[m], piece(x_in, me), x_send.at[1], x_recv.at[1], device_id={'kv': m}).start()

        piece(x_in, me)[...] = mid_out[me]

    def take_embeddings():
        all_pieces(1)
        y_ref[...] = x_in[...].reshape(d.tokens, d.width)

    plan_copy = pltpu.make_async_copy(plan_v, plan_s, plan_sem)

    def plan():
        seq = lax.broadcasted_iota(jnp.int32, (1, table_v.shape[1]), 1)
        worker = lax.rem(seq // d.rows + shift, group_size)
        before = lax.rem(worker + group_size - 1, group_size)
        first, last = table_v[0:1, :], table_v[1:2, :]
        bad = (last < worker * d.slots) | (last >= worker * d.slots + d.slots) | (first < before * d.slots) | (first >= before * d.slots + d.slots)

        def entry(e, state):
            plan, bad = state
            return jnp.where(last == dst_s[e], e, plan), bad | (first == dst_s[e]).astype(jnp.int32)

        plan, bad = lax.fori_loop(0, entries, entry, (jnp.full_like(last, -1), bad.astype(jnp.int32)))
        plan_v[...] = plan
        plan_copy.start()
        info_s[0] = shift
        info_s[1] = 1 - jnp.max(bad)

    def new_copies(l):
        return [pltpu.make_async_remote_copy(
            ref.at[pl.ds(g * d.stride + t * d.rows + half, half)], new_buf.at[l, p, g, t], new_send.at[l, p, g, t], new_recv.at[l, p, g, t], device_id={'kv': ahead})
            for p, ref in enumerate((dec.kn_s, dec.vn_s)) for g in range(d.kv_heads) for t in range(2)]

    def project(l):
        dec.project(l)
        for copy in new_copies(l):
            copy.start()

    scope("pack_0", pack, 0)
    step_0()
    scope("send_embeddings", send_embeddings)
    pages_0()
    scope("plan", plan)
    step_0()
    pages_0()
    step_0()
    pages_0()
    scope("pass_on", pass_on)
    step_0()
    pages_0()
    for l in range(1, d.layers):
        for load in pool_loads[l]:
            load.wait()
    step_0()
    pages_0()
    scope("own_1", own, 1)
    step_0()
    pages_0()
    scope("pack_1", pack, 1)
    step_0()
    pages_0()
    scope("take_embeddings", take_embeddings)
    step_1()
    step_0()
    pages_0()
    scope("project_0", project, 0)
    step_1()
    step_0()
    plan_copy.wait()
    step_0()
    scope("pages_wait_0", pages_wait, 0)

    def attend(l, events_a, events_b):
        def put_page(p, i, val):
            last_buf[p, i] = val

        dec.attend(lambda i: lens_s[home_a * d.rows + i], lambda p, i: got_buf[l, 0, p, i],
                   lambda p, i: migrated(l, p, home_a, i, last_here(l, p, i)), put_page, events_a, 0, half)
        dec.attend(lambda i: lens_s[home_b * d.rows + i], lambda p, i: first_here(l, p, i),
                   lambda p, i: migrated(l, p, home_b, i, got_buf[l, 1, p, i - half]), lambda p, i, val: None, events_b, half, half)
        dec.gather_heads()

    def finish_pages(l):
        for copy in new_copies(l):
            copy.wait()

        @pl.loop(0, half)
        def _(i):
            row = half + i
            for p in range(2):
                page = migrated(l, p, home_a, row, last_here(l, p, row))
                last_buf[p, row] = dec.insert(page, lens_s[home_a * d.rows + row], lambda t, g: new_buf[l, p, g, t, pl.ds(i, 1), :])

        pltpu.make_async_copy(last_buf, last_out.at[l], out_sem).start()

    def last_wait(l):
        pltpu.make_async_copy(last_buf, last_out.at[l], out_sem).wait()

    def event(run):
        return lambda: run()

    blocks = half // min(UNROLL, half)
    pairs = 2 * (d.n_u // 2)
    with jax.named_scope("attend_0"):
        attend(0, [(0, event(step_1))], [(0, event(step_1))])
    events = [((2 * k + 1) * pairs // (4 * parts), event(pages_1)) for k in range(2 * parts)]
    events += [(k * (pairs - 1) // 7, event(step_1)) for k in range(Exchange.STEPS - 4)]
    events += [(pairs - 1, functools.partial(scope, "finish_0", finish_pages, 0))]
    with jax.named_scope("mix_0"):
        dec.mix(0, sorted(events, key=lambda event: event[0]))
    for l in range(1, d.layers):
        scope(f"project_{l}", project, l)
        scope(f"pages_wait_{l}", pages_wait, l)
        last_wait(l - 1)
        with jax.named_scope(f"attend_{l}"):
            attend(l, [], [])
        with jax.named_scope(f"mix_{l}"):
            dec.mix(l, [(pairs // 2, functools.partial(finish_pages, l))])
    for t in range(2):
        ya_ref[t] = y_ref[pl.ds(t * d.rows, half), :]
        yb_ref[t] = y_ref[pl.ds(t * d.rows + half, half), :]
    last_wait(d.layers - 1)


def decode_adjacent(side, group_size, d, table, seq_lens, mig_src, mig_dst, embeds, weights, k_pool, v_pool):
    entries = mig_src.shape[0]
    half = d.rows // 2
    page = (d.page_rows, d.head_dim)
    struct = lambda *shape: jax.ShapeDtypeStruct(shape, BF16)
    groups = d.tokens // 8
    mid = pltpu.VMEM((group_size, 8, d.width * groups // group_size), BF16)
    return pl.pallas_call(
        functools.partial(adjacent_kernel, d, side, group_size, entries),
        out_shape=[struct(2, half, d.width), struct(2, half, d.width), jax.ShapeDtypeStruct((2,), jnp.int32), struct(d.layers, 2, d.rows, *page)],
        in_specs=[SMEM] * 2 + [ANY] * 11,
        out_specs=[VMEM, VMEM, SMEM, ANY],
        scratch_shapes=[
            pltpu.SMEM(table.shape, jnp.int32),
            pltpu.SMEM(seq_lens.shape, jnp.int32),
            pltpu.VMEM(table.shape, jnp.int32),
            pltpu.VMEM((groups, 8, d.width), BF16),
            pltpu.VMEM((d.tokens, d.width), BF16),
            pltpu.VMEM((d.layers, 2, 2, half) + page, BF16),
            pltpu.VMEM((d.layers, 2, 2, half) + page, BF16),
            pltpu.VMEM((2, d.rows) + page, BF16),
            pltpu.VMEM((d.layers, 2, d.kv_heads, 2, half, d.head_dim), F32),
            pltpu.VMEM((d.layers, 2 * entries) + page, BF16),
            pltpu.VMEM((d.layers, entries) + page, BF16),
            pltpu.VMEM((d.layers, entries) + page, BF16),
            mid,
            mid,
            pltpu.VMEM((groups, 8, d.width), BF16),
            pltpu.VMEM((1, table.shape[1]), jnp.int32),
            pltpu.SMEM((1, table.shape[1]), jnp.int32),
        ] + [pltpu.VMEM((2 * entries,) + page, BF16)] * d.layers + [pltpu.VMEM((d.slots,) + page, BF16)] * (2 * d.layers) + d.compute_scratch(10, 8) + [
            DMA((4,)),
            DMA((d.layers, 2)),
            DMA,
            DMA((2,)),
            DMA((2,)),
            DMA((d.layers, 2, 2)),
            DMA((d.layers, 2, 2)),
            DMA((d.layers, 2, d.kv_heads, 2)),
            DMA((d.layers, 2, d.kv_heads, 2)),
            DMA((d.layers, 10, 4)),
            DMA((d.layers, 10, 4)),
            DMA,
        ],
        compiler_params=pltpu.CompilerParams(collective_id=1, has_side_effects=True, skip_device_barrier=True, vmem_limit_bytes=LIMIT),
        cost_estimate=d.cost(d.layers),
        name="decode_adjacent",
    )(mig_src, mig_dst, table, seq_lens, embeds.reshape(groups, 8, d.width), *weights, k_pool, v_pool)


def fill_pools_kernel(dims, group_size, info_s, table_s, src_s, k_hbm, v_hbm, last_hbm, k_out, v_out, k_buf, v_buf, sem, put_sem):
    d = dims
    me = lax.axis_index('kv')
    home = lax.rem(me - info_s[0] + group_size, group_size)
    pools = ((k_hbm, k_buf, k_out), (v_hbm, v_buf, v_out))
    parts = sem.shape[1]
    size = d.slots // parts

    def moves(part, out):
        at = pl.ds(part * size, size)
        return [pltpu.make_async_copy(*((buf.at[at], dst.at[at]) if out else (src.at[at], buf.at[at])), sem.at[p, part]) for p, (src, buf, dst) in enumerate(pools)]

    def start(copies):
        for copy in copies:
            copy.start()

    def wait(copies):
        for copy in copies:
            copy.wait()

    def within(ids, count, part, run):
        @pl.loop(0, count)
        def _(i):
            slot = ids(i) - me * d.slots
            here = (slot >= part * size) & (slot < part * size + size)
            slot = jnp.clip(slot, 0, d.slots - 1)
            pl.when(here)(lambda: run(i, slot))

    def row_copies(i, slot):
        return [pltpu.make_async_copy(last_hbm.at[:, p, i], buf.at[slot], put_sem) for p, (_, buf, _) in enumerate(pools)]

    def clear(i, slot):
        for _, buf, _ in pools:
            buf[slot] = jnp.zeros(buf.shape[1:], buf.dtype)

    def last_id(i):
        return table_s[1, home * d.rows + i]

    @pl.loop(0, parts)
    def _(part):
        start(moves(part, False))

    @pl.loop(0, parts)
    def _(part):
        wait(moves(part, False))
        within(last_id, d.rows, part, lambda i, slot: start(row_copies(i, slot)))
        within(lambda e: src_s[e], src_s.shape[0], part, clear)
        within(last_id, d.rows, part, lambda i, slot: wait(row_copies(i, slot)))
        start(moves(part, True))

    @pl.loop(0, parts)
    def _(part):
        wait(moves(part, True))


def fill_pools(group_size, d, info, table, mig_src, k_pool, v_pool, last):
    size = 4 * k_pool.size
    return pl.pallas_call(
        functools.partial(fill_pools_kernel, d, group_size),
        out_shape=[jax.ShapeDtypeStruct(k_pool.shape, k_pool.dtype)] * 2,
        in_specs=[SMEM] * 3 + [ANY] * 3,
        out_specs=[ANY, ANY],
        scratch_shapes=[pltpu.VMEM(k_pool.shape, k_pool.dtype), pltpu.VMEM(k_pool.shape, k_pool.dtype), DMA((2, 4)), DMA],
        compiler_params=pltpu.CompilerParams(vmem_limit_bytes=LIMIT),
        cost_estimate=pl.CostEstimate(flops=40 * size, bytes_accessed=2 * size, transcendentals=0),
        name="fill_pools",
    )(info, table, mig_src, k_pool, v_pool, last)


def gather_pages_kernel(idx_ref, k_hbm, v_hbm, k_out, v_out, sem):
    rows = k_out.shape[0]

    def copies(i):
        slot = jnp.maximum(idx_ref[i], 0)
        return (pltpu.make_async_copy(k_hbm.at[slot], k_out.at[i], sem), pltpu.make_async_copy(v_hbm.at[slot], v_out.at[i], sem))

    @pl.loop(0, rows)
    def _(i):
        @pl.when(idx_ref[i] >= 0)
        def _():
            for copy in copies(i):
                copy.start()

        @pl.when(idx_ref[i] < 0)
        def _():
            k_out[i] = jnp.zeros(k_out.shape[1:], k_out.dtype)
            v_out[i] = jnp.zeros(v_out.shape[1:], v_out.dtype)

    @pl.loop(0, rows)
    def _(i):
        @pl.when(idx_ref[i] >= 0)
        def _():
            for copy in copies(i):
                copy.wait()


def gather_pages(idx, k_pool, v_pool):
    shape = jax.ShapeDtypeStruct((idx.shape[0],) + k_pool.shape[1:], k_pool.dtype)
    return pl.pallas_call(
        gather_pages_kernel,
        out_shape=[shape, shape],
        in_specs=[SMEM, ANY, ANY],
        out_specs=[VMEM, VMEM],
        scratch_shapes=[DMA],
        compiler_params=pltpu.CompilerParams(vmem_limit_bytes=LIMIT),
        name="gather_pages",
    )(idx, k_pool, v_pool)


def share_kernel(side, k_hbm, v_hbm, k_out, v_out, work, core_buf, ring_buf, load_sem, send_sem, recv_sem, result):
    entries = k_hbm.shape[0]
    exchange = Exchange(side, 0, work, core_buf, ring_buf, result, send_sem, recv_sem)
    units = [pl.ds(p * entries, entries) for p in range(2)]
    for p, src in enumerate((k_hbm, v_hbm)):
        pltpu.make_async_copy(src, work.at[0].at[units[p]], load_sem.at[p]).start()
    for p, src in enumerate((k_hbm, v_hbm)):
        pltpu.make_async_copy(src, work.at[0].at[units[p]], load_sem.at[p]).wait()
    for _ in range(Exchange.STEPS):
        exchange.step()
    for p, dst in enumerate((k_out, v_out)):
        pltpu.make_async_copy(result.at[units[p]], dst, load_sem.at[p]).start()
    for p, dst in enumerate((k_out, v_out)):
        pltpu.make_async_copy(result.at[units[p]], dst, load_sem.at[p]).wait()


def share(side, mig_k, mig_v):
    entries = mig_k.shape[0]
    page = mig_k.shape[1:]
    return pl.pallas_call(
        functools.partial(share_kernel, side),
        out_shape=[jax.ShapeDtypeStruct(mig_k.shape, BF16)] * 2,
        in_specs=[ANY, ANY],
        out_specs=[ANY, ANY],
        scratch_shapes=[pltpu.VMEM((1, n * entries) + page, BF16) for n in (2, 1, 1)] + [DMA((2,)), DMA((1, 10, 4)), DMA((1, 10, 4)), pltpu.VMEM((2 * entries,) + page, BF16)],
        compiler_params=pltpu.CompilerParams(has_side_effects=True, vmem_limit_bytes=LIMIT),
        name="share",
    )(mig_k, mig_v)


def migrate_kernel(dst_ref, src_ref, k_hbm, v_hbm, mk_hbm, mv_hbm, k_out, v_out, k_buf, v_buf, sem, fix_sem):
    entries = dst_ref.shape[0]
    pairs = ((k_hbm, mk_hbm, k_buf, k_out), (v_hbm, mv_hbm, v_buf, v_out))
    for p, (src, _, buf, _) in enumerate(pairs):
        pltpu.make_async_copy(src, buf, sem.at[p]).start()
    for p, (src, _, buf, _) in enumerate(pairs):
        pltpu.make_async_copy(src, buf, sem.at[p]).wait()

    @pl.loop(0, entries)
    def _(e):
        @pl.when(dst_ref[e] >= 0)
        def _():
            for _, mig, buf, _ in pairs:
                copy = pltpu.make_async_copy(mig.at[e], buf.at[jnp.maximum(dst_ref[e], 0)], fix_sem)
                copy.start()
                copy.wait()

        @pl.when(src_ref[e] >= 0)
        def _():
            for _, _, buf, _ in pairs:
                buf[jnp.maximum(src_ref[e], 0)] = jnp.zeros(buf.shape[1:], buf.dtype)

    for p, (_, _, buf, dst) in enumerate(pairs):
        pltpu.make_async_copy(buf, dst, sem.at[p]).start()
    for p, (_, _, buf, dst) in enumerate(pairs):
        pltpu.make_async_copy(buf, dst, sem.at[p]).wait()


def migrate(dst_local, src_local, k_pool, v_pool, mig_k, mig_v):
    shape = jax.ShapeDtypeStruct(k_pool.shape, k_pool.dtype)
    return pl.pallas_call(
        migrate_kernel,
        out_shape=[shape, shape],
        in_specs=[SMEM, SMEM, ANY, ANY, ANY, ANY],
        out_specs=[ANY, ANY],
        scratch_shapes=[pltpu.VMEM(k_pool.shape, k_pool.dtype), pltpu.VMEM(k_pool.shape, k_pool.dtype), DMA((2,)), DMA],
        compiler_params=pltpu.CompilerParams(vmem_limit_bytes=LIMIT),
        name="migrate",
    )(dst_local, src_local, k_pool, v_pool, mig_k, mig_v)


def decode_kernel(dims, sc_ref, x_ref, p0k_hbm, p0v_hbm, wq, wk, wv, wo, wu, wd, k_in, v_in, y_ref, k_out, v_out,
                  first_buf, last_buf, *rest):
    compute, (page_sem, put_sem) = rest[:-2], rest[-2:]
    d = dims
    dec = Decoder(d, 0, d.layers, (wq, wk, wv, wo, wu, wd), y_ref, compute, 1, 2)
    dec.start_stream()
    y_ref[...] = x_ref[...]
    loads = [pltpu.make_async_copy(src, first_buf.at[p], page_sem.at[p]) for p, src in enumerate((p0k_hbm, p0v_hbm))]
    for load in loads:
        load.start()

    def last_loads(run):
        @pl.loop(0, d.rows)
        def _(i):
            for p, src in enumerate((k_in, v_in)):
                run(pltpu.make_async_copy(src.at[sc_ref[0, i]], last_buf.at[p, i], page_sem.at[2]))

    def puts(run):
        @pl.loop(0, d.rows)
        def _(i):
            @pl.when(sc_ref[2, i] > 0)
            def _():
                for p, dst in enumerate((k_out, v_out)):
                    run(pltpu.make_async_copy(last_buf.at[p, i], dst.at[sc_ref[0, i]], put_sem))

    last_loads(lambda copy: copy.start())
    for load in loads:
        load.wait()
    last_loads(lambda copy: copy.wait())

    @pl.loop(0, d.layers)
    def _(layer):
        def put_page(p, i, val):
            last_buf[p, i, layer] = val

        dec.project(layer)
        dec.attend(lambda i: sc_ref[1, i], lambda p, i: first_buf[p, i, layer], lambda p, i: last_buf[p, i, layer], put_page)
        dec.gather_heads()
        dec.mix(layer)

    puts(lambda copy: copy.start())
    puts(lambda copy: copy.wait())


def decode(d, scalars, x, p0k, p0v, weights, k_pool, v_pool):
    pool = jax.ShapeDtypeStruct(k_pool.shape, k_pool.dtype)
    pages = pltpu.VMEM((2, d.rows, d.layers, d.page_rows, d.head_dim), BF16)
    return pl.pallas_call(
        functools.partial(decode_kernel, d),
        out_shape=[jax.ShapeDtypeStruct(x.shape, x.dtype), pool, pool],
        in_specs=[SMEM, VMEM] + [ANY] * 10,
        out_specs=[VMEM, ANY, ANY],
        input_output_aliases={10: 1, 11: 2},
        scratch_shapes=[pages, pages] + d.compute_scratch(16, 16) + [DMA((3,)), DMA],
        compiler_params=pltpu.CompilerParams(vmem_limit_bytes=LIMIT),
        cost_estimate=d.cost(d.layers),
        name="decode",
    )(scalars, x, p0k, p0v, *weights, k_pool, v_pool)


def permute(arrays, shift, group_size):
    if shift == group_size // 2:
        return permute(permute(arrays, shift // 2, group_size), shift // 2, group_size)
    perm = [(i, (i + shift) % group_size) for i in range(group_size)]
    return jax.tree.map(lambda a: lax.ppermute(a, 'kv', perm), arrays) if shift else arrays


def rotate_back(first, second, shift, group_size, beside):
    def branch(r):
        def run(args):
            parts = permute(args[0], -r % group_size, group_size), permute(args[1], (1 - r) % group_size, group_size)
            return jnp.concatenate(parts, axis=1), beside()

        return run

    return lax.switch(shift, [branch(r) for r in range(group_size)], (first, second))


def rotate(arrays, shift, group_size):
    stride = math.isqrt(2 * group_size)
    for count, move in ((shift // stride, stride), (shift % stride, 1)):
        arrays = lax.fori_loop(0, count, lambda _, a: permute(a, move, group_size), arrays)
    return arrays


def solution(mesh):
    group_size = mesh.shape['kv']
    side = math.isqrt(group_size // 2)
    pool_spec = P(('rep', 'kv'))
    tok_spec = P(None, ('rep', 'kv'), None)

    def device_fn(embeds, w_query, w_key, w_value, w_out, w_up, w_down, k_pool5, v_pool5, new_table, seq_lens, mig_src, mig_dst):
        me = lax.axis_index('kv')
        slots, layers, page, kv_heads, head_dim = k_pool5.shape
        rows, width = embeds.shape[1:]
        weights = (w_query, w_key, w_value, w_out, w_up, w_down)
        k_pool = k_pool5.reshape(slots, layers, page * kv_heads, head_dim)
        v_pool = v_pool5.reshape(slots, layers, page * kv_heads, head_dim)
        d = Dims(rows, weights, k_pool, page)
        ints = jnp.int32

        def local(ids):
            loc = ids - me * slots
            return jnp.where((loc >= 0) & (loc < slots), loc, -1)

        def take(vec, dev):
            return lax.dynamic_slice(vec, (dev * rows,), (rows,))

        def inside(ids):
            return jnp.clip(ids - me * slots, 0, slots - 1)

        def general_path():
            first_new, last_new = new_table[:, 0], new_table[:, 1]
            moved = first_new[None, :] == mig_dst[:, None]
            first_old = jnp.where(jnp.any(moved, axis=0), jnp.sum(jnp.where(moved, mig_src[:, None], 0), axis=0), first_new)
            home = jnp.arange(first_new.shape[0], dtype=ints) // rows
            worker = last_new // slots
            shift_of = (worker - home + group_size) % group_size
            first_shift = (worker - first_old // slots + group_size) % group_size
            shift_ids = jnp.arange(group_size, dtype=ints)
            wanted = jnp.any(shift_of[None, :] == shift_ids[:, None], axis=1)
            mig_k, mig_v = gather_pages(local(mig_src), k_pool, v_pool)
            by_layer = tuple(m.swapaxes(0, 1) for m in (mig_k, mig_v))
            mig_k, mig_v = (m.swapaxes(0, 1) for m in lax.map(lambda pages: tuple(share(side, *pages)), by_layer))
            k_new, v_new = migrate(local(mig_dst), local(mig_src), k_pool, v_pool, mig_k, mig_v)

            def one_round(shift, y, k_new, v_new):
                src_home = (me - shift + group_size) % group_size
                x = rotate(embeds.reshape(2 * rows, width), shift, group_size)
                in_round = shift_of == shift
                wanted2 = jnp.any(in_round[None, :] & (first_shift[None, :] == shift_ids[:, None]), axis=1)

                def more(state):
                    left, pk, pv = state
                    shift2 = jnp.argmax(left).astype(ints)
                    dest_home = (me + shift2 - shift + group_size) % group_size
                    got = gather_pages(inside(take(first_old, dest_home)), k_pool, v_pool)
                    got_k, got_v = rotate(tuple(got), shift2, group_size)
                    mine = (take(first_shift, src_home) == shift2)[:, None, None, None]
                    return left & (shift_ids != shift2), jnp.where(mine, got_k, pk), jnp.where(mine, got_v, pv)

                zeros = jnp.zeros((rows,) + k_pool.shape[1:], k_pool.dtype)
                _, pk, pv = lax.while_loop(lambda state: jnp.any(state[0]), more, (wanted2, zeros, zeros))
                valid = take(shift_of, src_home) == shift
                scalars = jnp.stack([inside(take(last_new, src_home)), take(seq_lens, src_home), valid.astype(ints)])
                out, k_new, v_new = decode(d, scalars, x, pk, pv, weights, k_new, v_new)
                back = rotate(out, (group_size - shift) % group_size, group_size)
                mine = (take(shift_of, me) == shift)[None, :, None]
                return jnp.where(mine, back.reshape(embeds.shape), y), k_new, v_new

            def next_round(state):
                left, y, k_new, v_new = state
                shift = jnp.argmax(left).astype(ints)
                y, k_new, v_new = one_round(shift, y, k_new, v_new)
                return left & (shift_ids != shift), y, k_new, v_new

            _, y, k_new, v_new = lax.while_loop(lambda state: jnp.any(state[0]), next_round, (wanted, jnp.zeros_like(embeds), k_new, v_new))
            return y, k_new, v_new

        table = new_table.T
        ya, yb, info, last = decode_adjacent(side, group_size, d, table, seq_lens, mig_src, mig_dst, embeds, weights, k_pool, v_pool)
        y, (k_new, v_new) = rotate_back(ya, yb, info[0], group_size, lambda: fill_pools(group_size, d, info, table, mig_src, k_pool, v_pool, last))
        _, y, k_new, v_new = lax.while_loop(lambda state: state[0] == 0, lambda state: (jnp.ones_like(state[0]),) + general_path(), (info[1], y, k_new, v_new))
        return y, k_new.reshape(k_pool5.shape), v_new.reshape(v_pool5.shape)

    return jax.shard_map(device_fn, mesh=mesh, in_specs=(tok_spec, P(), P(), P(), P(), P(), P(), pool_spec, pool_spec, P('rep', None), P('rep'), P('rep'), P('rep')), out_specs=(tok_spec, pool_spec, pool_spec), check_vma=False)
```

profile of v0, /device:TPU:97, one launch (start us, length us, event | category | flops | bytes accessed | tf_op | source)
XLA Modules:
  0.0 162.7 jit_solution(433067718159151496)
XLA Ops:
  0.6 0.0 copy-start.3
  0.6 135.7 %decode_adjacent.1 = (bf16[2,32,2048]{2,1,0:T(8,128)(2,1)S(1)}, bf16[2,32,2048]{2,1,0:T(8,128)(2,1)S(1)}, s32[2]{0:T(128)S(1)}, bf16[2,2,64,64,128]{4,3,2,1,0:T(8,128)(2,1)}) custom-call(s32[64]{0:T(128)} %src_s.1, s32[64]{0:T(128)} %dst_s.1, s32[2,2048]{1,0:T(2,128)} %bitcast.129, s32[2048]{0:T(1024)} %lens_hbm.1, bf16[16,8,2048]{2,1,0:T(8,128)(2,1)} %bitcast.122, ...), custom_call_target="tpu_custom_call" | custom-call | flops 27917287424 | bytes 218103808 | tf_op jit(solution)/shard_map/decode_adjacent/pallas_call | solution.py:644
  136.4 0.6 fusion.19
  137.6 0.0 copy-done.3
  137.6 0.0 copy-start.39
  137.6 23.1 %conditional.1 = (bf16[2,64,2048]{2,1,0:T(8,128)(2,1)S(1)}, bf16[192,2,64,128]{3,2,1,0:T(8,128)(2,1)}, bf16[192,2,64,128]{3,2,1,0:T(8,128)(2,1)}) conditional(s32[]{:T(128)} %bitcast.15, (bf16[2,32,2048]{2,1,0:T(8,128)(2,1)S(1)}, bf16[2,32,2048]{2,1,0:T(8,128)(2,1)S(1)}, s32[2]{0:T(128)S(1)}, ...), branch_computations={%region_0.0_spmd, %region_1.0_spmd, %region_2.0_spmd, %region_3.0_... | conditional | flops 504365056 | bytes 30408876 | solution.py:942
  137.9 3.7 %collective-permute-start.40 = (bf16[2,32,2048]{2,1,0:T(8,128)(2,1)S(1)}, bf16[2,32,2048]{2,1,0:T(8,128)(2,1)S(1)}, u32[]{:S(2)}, u32[]{:S(2)}) collective-permute-start(bf16[2,32,2048]{2,1,0:T(8,128)(2,1)S(1)} %get-tuple-element.1533), channel_id=1, source_target_pairs={{0,12},{1,13},{2,14},{3,15},{4,16},{5,17},{6,18},{7,19},{8,20},{9,... | collective-permute-start | bytes 786440 | tf_op jit(solution)/shard_map/cond/branch_20_fun/ppermute | solution.py:931
  141.6 1.9 %collective-permute-start.41 = (bf16[2,32,2048]{2,1,0:T(8,128)(2,1)S(1)}, bf16[2,32,2048]{2,1,0:T(8,128)(2,1)}, u32[]{:S(2)}, u32[]{:S(2)}) collective-permute-start(bf16[2,32,2048]{2,1,0:T(8,128)(2,1)S(1)} %get-tuple-element.1534), channel_id=1, source_target_pairs={{0,13},{1,14},{2,15},{3,16},{4,17},{5,18},{6,19},{7,20},{8,21},{9,... | collective-permute-start | bytes 786440 | tf_op jit(solution)/shard_map/cond/branch_20_fun/ppermute | solution.py:931
  143.5 15.4 %fill_pools.52 = (bf16[192,2,64,128]{3,2,1,0:T(8,128)(2,1)}, bf16[192,2,64,128]{3,2,1,0:T(8,128)(2,1)}) custom-call(s32[2]{0:T(128)S(1)} %get-tuple-element.1535.info_s, s32[2,2048]{1,0:T(2,128)S(1)} %get-tuple-element.1536.table_s, s32[64]{0:T(128)} %get-tuple-element.1537.src_s, bf16[192,2,64,128]{3,2,1,0:T(8,128)(2,1)} %get-tuple-element.1538.k_hbm, ...), custom_call_target="tpu_custom_call" | custom-call | flops 503316480 | bytes 25165824 | tf_op jit(solution)/shard_map/cond/branch_20_fun/fill_pools/pallas_call | solution.py:744
  158.9 0.0 collective-permute-done.40
  158.9 0.0 copy-start.25
  159.0 0.7 copy-done.25
  159.7 0.0 collective-permute-done.41
  159.7 1.1 pad_maximum_fusion.20
  160.8 0.0 copy-start
  160.8 0.8 copy-done
  161.6 0.0 copy-done.39
  161.6 0.9 while.201
Async XLA Ops:
  0.6 137.0 %copy-start.3 = (s32[2048,2]{0,1:T(2,128)S(1)}, s32[2048,2]{0,1:T(2,128)}, u32[]{:S(2)}) copy-start(s32[2048,2]{0,1:T(2,128)} %param.74) | copy-start | bytes 49156
  137.6 23.9 %copy-start.39 = (s32[64]{0:T(128)S(1)}, s32[64]{0:T(128)}, u32[]{:S(2)}) copy-start(s32[64]{0:T(128)} %dst_s.1) | copy-start | bytes 772
  137.9 21.0 %collective-permute-start.40 = (bf16[2,32,2048]{2,1,0:T(8,128)(2,1)S(1)}, bf16[2,32,2048]{2,1,0:T(8,128)(2,1)S(1)}, u32[]{:S(2)}, u32[]{:S(2)}) collective-permute-start(bf16[2,32,2048]{2,1,0:T(8,128)(2,1)S(1)} %get-tuple-element.1533), channel_id=1, source_target_pairs={{0,12},{1,13},{2,14},{3,15},{4,16},{5,17},{6,18},{7,19},{8,20},{9,... | collective-permute-start | bytes 786440 | tf_op jit(solution)/shard_map/cond/branch_20_fun/ppermute | solution.py:931
  141.6 18.1 %collective-permute-start.41 = (bf16[2,32,2048]{2,1,0:T(8,128)(2,1)S(1)}, bf16[2,32,2048]{2,1,0:T(8,128)(2,1)}, u32[]{:S(2)}, u32[]{:S(2)}) collective-permute-start(bf16[2,32,2048]{2,1,0:T(8,128)(2,1)S(1)} %get-tuple-element.1534), channel_id=1, source_target_pairs={{0,13},{1,14},{2,15},{3,16},{4,17},{5,18},{6,19},{7,20},{8,21},{9,... | collective-permute-start | bytes 786440 | tf_op jit(solution)/shard_map/cond/branch_20_fun/ppermute | solution.py:931
  158.9 0.7 copy-start.25
  160.8 0.8 copy-start
where the time goes:
time: 162 us; the launch traced here: 163 us
  Pallas kernels  151 us (93%)
  starting transfers between devices  5.58 us (3%)
  local copies, waits for them, and re-layouts  2.1 us (1%)
    pallas_call x1, Pallas kernels, decode_adjacent(): pl.pallas_call(functools.partial(adjacent_kernel, d, side, group_size, en...  136 us
    pallas_call x1, Pallas kernels, fill_pools(): pl.pallas_call(functools.partial(fill_pools_kernel, d, group_size), out_s...  15.4 us
    ppermute x2, starting transfers between devices, permute(): lax.ppermute(a, 'kv', perm)  5.58 us
  transfers between devices with their start and end apart: 2, of which 0 were waited for; matrix products, arithmetic and copies ran while one was open for 0% of the time, Pallas kernels for 9%

commit v1 on v0

--- a/solution.py
+++ b/solution.py
@@ -14,8 +14,23 @@
 DMA = pltpu.SemaphoreType.DMA
 CHUNK = 256
 UNROLL = 8
+LANES = 128
+HALF = CHUNK // 2
+PAIR = (0, 1)
 LIMIT = 63 << 20
 F32, BF16 = jnp.float32, jnp.bfloat16
+
+
+def iota(shape, axis):
+    return lax.broadcasted_iota(jnp.int32, shape, axis)
+
+
+def dot(a, b):
+    return jnp.dot(a, b, preferred_element_type=F32)
+
+
+def local_slot(ids, me, slots):
+    return jnp.clip(ids - me * slots, 0, slots - 1)
 
 
 def aligned(x, multiple):
@@ -57,20 +72,23 @@
 
 
 class Decoder:
-    def __init__(self, dims, first, layers, weights, y_ref, scratch, group=2, unroll=UNROLL):
-        self.group, self.unroll = group, unroll
+    def __init__(self, dims, first, layers, weights, y_ref, scratch, group=2, unroll=UNROLL, shared=False):
+        self.group, self.unroll, self.shared = group, unroll, shared
         self.d, self.first, self.layers, self.weights, self.y_ref = dims, first, layers, weights, y_ref
         (self.col_buf, self.row_buf, self.q_s, self.kn_s, self.vn_s, self.o_s, self.att, self.act, self.acc, self.col_sem, self.row_sem) = scratch
         self.n_col, self.n_row = self.col_buf.shape[0], self.row_buf.shape[0]
         self.zero = lax.axis_index('kv') * 0
         d = dims
+        self.whole, self.begin = d.ff // 2 // CHUNK, lax.axis_index('kv') % 2 * (d.ff // 2)
+        self.cols = layers * d.col_layer - shared * (d.n_u - self.whole)
+        self.downs = layers * d.n_u - shared * (d.n_u - self.whole)
         cols = 2 * d.page * d.kv_heads
-        col_pos = lax.broadcasted_iota(jnp.int32, (2 * d.heads, cols), 1)
-        row_pos = lax.broadcasted_iota(jnp.int32, (2 * d.heads, cols), 0)
+        col_pos = iota((2 * d.heads, cols), 1)
+        row_pos = iota((2 * d.heads, cols), 0)
         same_head = (col_pos % d.kv_heads) == (row_pos % d.heads) // (d.heads // d.kv_heads)
         self.limit = jnp.where(same_head, col_pos // d.kv_heads - row_pos // d.heads, 4 * d.page)
-        self.page_pos = lax.broadcasted_iota(jnp.int32, (d.page_rows, d.head_dim), 0) // d.kv_heads
-        self.tile_head = lax.broadcasted_iota(jnp.int32, (8, d.head_dim), 0) % d.kv_heads
+        self.page_pos = iota((d.page_rows, d.head_dim), 0) // d.kv_heads
+        self.tile_head = iota((8, d.head_dim), 0) % d.kv_heads
 
     def layer_of(self, g, per_layer):
         return sum((g >= per_layer * l).astype(jnp.int32) for l in range(1, self.layers))
@@ -79,14 +97,14 @@
         d = self.d
         wq, wk, wv, wo, wu, _ = self.weights
 
-        @pl.when(g < self.layers * d.col_layer)
+        @pl.when(g < self.cols)
         def _():
             layer = self.layer_of(g, d.col_layer)
             pos = g - layer * d.col_layer
             slot = g % self.n_col
 
-            def go(src, c):
-                start = aligned(c * CHUNK, CHUNK)
+            def go(src, c, begin=0):
+                start = aligned(c * CHUNK + begin, LANES)
                 pltpu.make_async_copy(src.at[self.first + layer].at[:, pl.ds(start, CHUNK)], self.col_buf.at[slot], self.col_sem.at[slot]).start()
 
             @pl.when(pos < d.n_q)
@@ -107,17 +125,17 @@
 
             @pl.when(pos >= d.n_q + 2 + d.n_o)
             def _():
-                go(wu, pos - (d.n_q + 2 + d.n_o))
+                go(wu, pos - (d.n_q + 2 + d.n_o), self.begin * (layer == self.layers - 1) if self.shared else 0)
 
     def row_start(self, g):
         d = self.d
         wd = self.weights[5]
 
-        @pl.when(g < self.layers * d.n_u)
+        @pl.when(g < self.downs)
         def _():
             layer = self.layer_of(g, d.n_u)
             slot = g % self.n_row
-            start = aligned((g - layer * d.n_u) * CHUNK, CHUNK)
+            start = aligned((g - layer * d.n_u) * CHUNK + (self.begin * (layer == self.layers - 1) if self.shared else 0), LANES)
             pltpu.make_async_copy(wd.at[self.first + layer].at[pl.ds(start, CHUNK)], self.row_buf.at[slot], self.row_sem.at[slot]).start()
 
     def start_stream(self):
@@ -150,7 +168,7 @@
         col0 = (self.zero + layer) * d.col_layer
 
         def product(ref):
-            return jnp.dot(self.y_ref[...], ref[...], preferred_element_type=F32).astype(BF16).astype(F32)
+            return dot(self.y_ref[...], ref[...]).astype(BF16).astype(F32)
 
         def put(dst, first, out):
             for h in range(CHUNK // d.head_dim):
@@ -178,7 +196,7 @@
     def insert(self, page, n, row):
         d = self.d
         val = page.astype(F32)
-        for t in range(2):
+        for t in PAIR:
             new = jnp.broadcast_to(row(t, 0), (8, d.head_dim))
             for g in range(1, d.kv_heads):
                 new = jnp.where(self.tile_head == g, row(t, g), new)
@@ -203,7 +221,7 @@
 
                 keys = jnp.concatenate([first_page(0, i), updated(0, self.kn_s)], axis=0)
                 vals.append(updated(1, self.vn_s))
-                qs = jnp.concatenate([self.q_s[pl.ds(t * d.rows + i, d.heads, stride=d.stride), :] for t in range(2)], axis=0)
+                qs = jnp.concatenate([self.q_s[pl.ds(t * d.rows + i, d.heads, stride=d.stride), :] for t in PAIR], axis=0)
                 score = lax.dot_general(qs.astype(BF16), keys, (((1,), (1,)), ((), ())), preferred_element_type=F32) * d.head_dim ** -0.5
                 scores.append(jnp.where(self.limit <= n, score, -jnp.inf))
             tops = [jnp.max(score, axis=1, keepdims=True) for score in scores]
@@ -211,8 +229,8 @@
             totals = [jnp.sum(prob, axis=1, keepdims=True) for prob in probs]
             for u, i in enumerate(ids):
                 both = jnp.concatenate([first_page(1, i), vals[u]], axis=0)
-                out = jnp.dot(probs[u].astype(BF16), both, preferred_element_type=F32) / totals[u]
-                for t in range(2):
+                out = dot(probs[u].astype(BF16), both) / totals[u]
+                for t in PAIR:
                     self.o_s[pl.ds(t * d.rows + i, d.heads, stride=d.stride), :] = out[t * d.heads:(t + 1) * d.heads]
 
         @pl.loop(0, count // unroll)
@@ -225,6 +243,24 @@
         d = self.d
         for h in range(d.heads):
             self.att[:, h * d.head_dim:(h + 1) * d.head_dim] = self.o_s[h * d.stride:h * d.stride + d.tokens, :].astype(BF16)
+
+    def span(self, j):
+        return pl.ds(aligned(j * CHUNK, CHUNK), CHUNK)
+
+    def out_project(self, layer, after=None):
+        d, many = self.d, self.group
+
+        @pl.loop(0, d.n_o // many)
+        def _(j):
+            def body(refs):
+                outs = [dot(self.att[...], ref[...]) for ref in refs]
+                for u in range(many):
+                    at = self.span(many * j + u)
+                    self.y_ref[:, at] = (self.y_ref[:, at].astype(F32) + outs[u]).astype(BF16)
+
+            self.with_cols(layer * d.col_layer + d.n_q + len(PAIR) + many * j, many, body)
+            if after:
+                after(j)
 
     def mix(self, layer, events=()):
         d = self.d
@@ -238,24 +274,13 @@
                 if first <= k < first + pairs:
                     pl.when(j == k - first)(run)
 
-        def span(j):
-            return pl.ds(aligned(j * CHUNK, CHUNK), CHUNK)
-
-        @pl.loop(0, d.n_o // many)
-        def _(j):
-            def body(refs):
-                outs = [jnp.dot(self.att[...], ref[...], preferred_element_type=F32) for ref in refs]
-                for u in range(many):
-                    at = span(many * j + u)
-                    self.y_ref[:, at] = (self.y_ref[:, at].astype(F32) + outs[u]).astype(BF16)
-
-            self.with_cols(col0 + many * j, many, body)
+        self.out_project(layer)
 
         def up(first, count):
             def body(refs):
-                ups = [jnp.dot(self.y_ref[...], ref[...], preferred_element_type=F32) for ref in refs]
+                ups = [dot(self.y_ref[...], ref[...]) for ref in refs]
                 for u in range(count):
-                    self.act[:, span(first + u)] = jax.nn.gelu(ups[u].astype(BF16).astype(F32), approximate=True).astype(BF16)
+                    self.act[:, self.span(first + u)] = jax.nn.gelu(ups[u].astype(BF16).astype(F32), approximate=True).astype(BF16)
 
             self.with_cols(col0 + d.n_o + first, count, body)
 
@@ -263,7 +288,7 @@
             def body(refs):
                 out = self.acc[...]
                 for u in range(count):
-                    out += jnp.dot(self.act[:, span(first + u)], refs[u][...], preferred_element_type=F32)
+                    out += dot(self.act[:, self.span(first + u)], refs[u][...])
                 self.acc[...] = out
 
             self.with_rows(layer * d.n_u + first, count, body)
@@ -287,6 +312,78 @@
             down(d.n_u - 1, 1)
 
         self.y_ref[...] = self.acc[...].astype(BF16)
+
+
+    def half_start(self):
+        layer, at = self.first + self.layers - 1, pl.ds(aligned(self.begin + self.whole * CHUNK, LANES), HALF)
+        return (pltpu.make_async_copy(self.weights[4].at[layer].at[:, at], self.half_col, self.half_sem.at[0]),
+                pltpu.make_async_copy(self.weights[5].at[layer].at[at], self.half_row, self.half_sem.at[1]))
+
+    def mix_shared(self, layer, send_hidden, wait_hidden, swap_sums, events=()):
+        d = self.d
+        layer = self.zero + layer
+        col0 = layer * d.col_layer + d.n_q + 2
+        many = self.group
+        rows = d.tokens
+        offset = d.ff // 2
+
+        self.out_project(layer, send_hidden)
+
+        self.acc[...] = self.y_ref[...].astype(F32)
+        self.acc_other[...] = jnp.zeros_like(self.acc_other)
+        wait_hidden()
+
+        def hidden():
+            return jnp.concatenate([self.y_ref[...], self.y_other[...]], axis=0)
+
+        def activate(up, at, size):
+            val = jax.nn.gelu(up.astype(BF16).astype(F32), approximate=True).astype(BF16)
+            self.act[:, pl.ds(aligned(at, LANES), size)] = val[:rows]
+            self.act[:, pl.ds(aligned(at + offset, LANES), size)] = val[rows:]
+
+        @pl.loop(0, self.whole // many)
+        def _(j):
+            for k, run in events:
+                pl.when(j == k)(run)
+
+            def body(refs):
+                ups = [dot(hidden(), ref[...]) for ref in refs]
+                for u in range(many):
+                    activate(ups[u], (many * j + u) * CHUNK, CHUNK)
+
+            self.with_cols(col0 + d.n_o + many * j, many, body)
+
+        tail = self.whole % many
+        for u in range(tail):
+            def body(refs, at=(self.whole - tail + u) * CHUNK):
+                activate(dot(hidden(), refs[0][...]), at, CHUNK)
+
+            self.with_cols(col0 + d.n_o + self.whole - tail + u, 1, body)
+        for copy in self.half_start():
+            copy.wait()
+        activate(dot(hidden(), self.half_col[...]), self.whole * CHUNK, HALF)
+
+        def acts(at, size):
+            return jnp.concatenate([self.act[:, pl.ds(aligned(at, LANES), size)], self.act[:, pl.ds(aligned(at + offset, LANES), size)]], axis=0)
+
+        def add(out):
+            self.acc[...] += out[:rows]
+            self.acc_other[...] += out[rows:]
+
+        @pl.loop(0, self.whole // many)
+        def _(j):
+            def body(refs):
+                add(sum(dot(acts((many * j + u) * CHUNK, CHUNK), refs[u][...]) for u in range(many)))
+
+            self.with_rows(layer * d.n_u + many * j, many, body)
+
+        for u in range(tail):
+            def body(refs, at=(self.whole - tail + u) * CHUNK):
+                add(dot(acts(at, CHUNK), refs[0][...]))
+
+            self.with_rows(layer * d.n_u + self.whole - tail + u, 1, body)
+        add(dot(acts(self.whole * CHUNK, HALF), self.half_row[...]))
+        self.y_ref[...] = (self.acc[...] + swap_sums()).astype(BF16)
 
 
 class Exchange:
@@ -378,15 +475,16 @@
 
 def adjacent_kernel(dims, side, group_size, entries, src_s, dst_s, table_hbm, lens_hbm, embeds_hbm, wq, wk, wv, wo, wu, wd, k_hbm, v_hbm,
                     ya_ref, yb_ref, info_s, last_out,
-                    table_s, lens_s, table_v, embeds_v, y_ref, send_buf, got_buf, last_buf, new_buf, work, core_buf, ring_buf, mid_in, mid_out, x_in, plan_v, plan_s, *rest):
+                    table_s, lens_s, table_v, embeds_v, y_ref, send_buf, got_buf, last_buf, new_buf, work, core_buf, ring_buf, mid_in, mid_out, x_in, plan_v, plan_s, y_other, acc_other, sums_in, half_col, half_row, *rest):
     d = dims
     migs, rest = rest[:d.layers], rest[d.layers:]
     pools, rest = [rest[2 * l:2 * l + 2] for l in range(d.layers)], rest[2 * d.layers:]
-    compute, (load_sem, pool_sem, plan_sem, x_send, x_recv, page_send, page_recv, new_send, new_recv, mig_send, mig_recv, out_sem) = rest[:-12], rest[-12:]
+    compute, (load_sem, pool_sem, plan_sem, x_send, x_recv, page_send, page_recv, new_send, new_recv, mig_send, mig_recv, out_sem, half_sem, pair_send, pair_recv) = rest[:-15], rest[-15:]
     half = d.rows // 2
     me = lax.axis_index('kv')
     ahead, behind = lax.rem(me + 1, group_size), lax.rem(me + group_size - 1, group_size)
-    dec = Decoder(d, 0, d.layers, (wq, wk, wv, wo, wu, wd), y_ref, compute)
+    dec = Decoder(d, 0, d.layers, (wq, wk, wv, wo, wu, wd), y_ref, compute, shared=True)
+    dec.y_other, dec.acc_other, dec.half_col, dec.half_row, dec.half_sem = y_other, acc_other, half_col, half_row, half_sem
     exchanges = [Exchange(side, l, work, core_buf, ring_buf, migs[l], mig_send, mig_recv) for l in range(d.layers)]
 
     def scope(name, run, *args):
@@ -439,8 +537,8 @@
         def _(e):
             slot = src_s[e] - me * d.slots
             mine = (slot >= 0) & (slot < d.slots)
-            slot = jnp.clip(slot, 0, d.slots - 1)
-            for p in range(2):
+            slot = local_slot(src_s[e], me, d.slots)
+            for p in PAIR:
                 page = pools[l][p][slot]
                 work[l, p * entries + e] = jnp.where(mine, page, jnp.zeros_like(page))
 
@@ -455,12 +553,14 @@
         for load in pool_loads[l]:
             load.start()
     scope("start_stream", dec.start_stream)
+    for copy in dec.half_start():
+        copy.start()
     shift = scope("load_tables", load_tables)
     home_a = lax.rem(me - shift + group_size, group_size)
     home_b = lax.rem(home_a + 1, group_size)
 
     def clipped(slot):
-        return jnp.clip(slot - me * d.slots, 0, d.slots - 1)
+        return local_slot(slot, me, d.slots)
 
     def first_here(l, p, i):
         return pools[l][p][clipped(table_s[0, home_b * d.rows + i])]
@@ -475,7 +575,7 @@
     def pack(l):
         @pl.loop(0, half)
         def _(i):
-            for p in range(2):
+            for p in PAIR:
                 send_buf[l, 0, p, i] = first_here(l, p, i)
                 send_buf[l, 1, p, i] = last_here(l, p, half + i)
 
@@ -486,18 +586,18 @@
         return pltpu.make_async_remote_copy(
             send_buf.at[l, way, p, rows], got_buf.at[l, way, p, rows], page_send.at[l, way, p], page_recv.at[l, way, p], device_id={'kv': (ahead, behind)[way]})
 
-    pieces = [iter([(p, part) for part in range(parts) for p in range(2)]) for _ in range(d.layers)]
+    pieces = [iter([(p, part) for part in range(parts) for p in PAIR]) for _ in range(d.layers)]
 
     def pages_start(l):
         p, part = next(pieces[l])
-        for way in range(2):
+        for way in PAIR:
             page_copy(l, way, p, pl.ds(part * size, size)).start()
 
     pages_0, pages_1 = functools.partial(pages_start, 0), functools.partial(pages_start, 1)
 
     def pages_wait(l):
-        for way in range(2):
-            for p in range(2):
+        for way in PAIR:
+            for p in PAIR:
                 page_copy(l, way, p, pl.ds(0, half)).wait()
 
     def pass_on():
@@ -522,7 +622,7 @@
     plan_copy = pltpu.make_async_copy(plan_v, plan_s, plan_sem)
 
     def plan():
-        seq = lax.broadcasted_iota(jnp.int32, (1, table_v.shape[1]), 1)
+        seq = iota((1, table_v.shape[1]), 1)
         worker = lax.rem(seq // d.rows + shift, group_size)
         before = lax.rem(worker + group_size - 1, group_size)
         first, last = table_v[0:1, :], table_v[1:2, :]
@@ -541,7 +641,7 @@
     def new_copies(l):
         return [pltpu.make_async_remote_copy(
             ref.at[pl.ds(g * d.stride + t * d.rows + half, half)], new_buf.at[l, p, g, t], new_send.at[l, p, g, t], new_recv.at[l, p, g, t], device_id={'kv': ahead})
-            for p, ref in enumerate((dec.kn_s, dec.vn_s)) for g in range(d.kv_heads) for t in range(2)]
+            for p, ref in enumerate((dec.kn_s, dec.vn_s)) for g in range(d.kv_heads) for t in PAIR]
 
     def project(l):
         dec.project(l)
@@ -599,7 +699,7 @@
         @pl.loop(0, half)
         def _(i):
             row = half + i
-            for p in range(2):
+            for p in PAIR:
                 page = migrated(l, p, home_a, row, last_here(l, p, row))
                 last_buf[p, row] = dec.insert(page, lens_s[home_a * d.rows + row], lambda t, g: new_buf[l, p, g, t, pl.ds(i, 1), :])
 
@@ -620,15 +720,34 @@
     events += [(pairs - 1, functools.partial(scope, "finish_0", finish_pages, 0))]
     with jax.named_scope("mix_0"):
         dec.mix(0, sorted(events, key=lambda event: event[0]))
+    def hidden_copy(at):
+        return pltpu.make_async_remote_copy(y_ref.at[:, at], y_other.at[:, at], pair_send.at[0], pair_recv.at[0], device_id={'kv': exchanges[0].partner})
+
+    def send_hidden(j):
+        hidden_copy(pl.ds(aligned(j * dec.group * CHUNK, CHUNK), dec.group * CHUNK)).start()
+
+    def wait_hidden():
+        hidden_copy(pl.ds(0, d.width)).wait()
+
+    def swap_sums():
+        copy = pltpu.make_async_remote_copy(acc_other, sums_in, pair_send.at[1], pair_recv.at[1], device_id={'kv': exchanges[0].partner})
+        copy.start()
+        copy.wait()
+        return sums_in[...]
+
     for l in range(1, d.layers):
         scope(f"project_{l}", project, l)
         scope(f"pages_wait_{l}", pages_wait, l)
         last_wait(l - 1)
         with jax.named_scope(f"attend_{l}"):
             attend(l, [], [])
+        finish = [(1, functools.partial(finish_pages, l))]
         with jax.named_scope(f"mix_{l}"):
-            dec.mix(l, [(pairs // 2, functools.partial(finish_pages, l))])
-    for t in range(2):
+            if l == d.layers - 1:
+                dec.mix_shared(l, send_hidden, wait_hidden, swap_sums, finish)
+            else:
+                dec.mix(l, finish)
+    for t in PAIR:
         ya_ref[t] = y_ref[pl.ds(t * d.rows, half), :]
         yb_ref[t] = y_ref[pl.ds(t * d.rows + half, half), :]
     last_wait(d.layers - 1)
@@ -652,32 +771,26 @@
             pltpu.VMEM(table.shape, jnp.int32),
             pltpu.VMEM((groups, 8, d.width), BF16),
             pltpu.VMEM((d.tokens, d.width), BF16),
-            pltpu.VMEM((d.layers, 2, 2, half) + page, BF16),
-            pltpu.VMEM((d.layers, 2, 2, half) + page, BF16),
+        ] + [pltpu.VMEM((d.layers, 2, 2, half) + page, BF16)] * len(PAIR) + [
             pltpu.VMEM((2, d.rows) + page, BF16),
             pltpu.VMEM((d.layers, 2, d.kv_heads, 2, half, d.head_dim), F32),
             pltpu.VMEM((d.layers, 2 * entries) + page, BF16),
-            pltpu.VMEM((d.layers, entries) + page, BF16),
-            pltpu.VMEM((d.layers, entries) + page, BF16),
+        ] + [pltpu.VMEM((d.layers, entries) + page, BF16)] * len(PAIR) + [
             mid,
             mid,
             pltpu.VMEM((groups, 8, d.width), BF16),
             pltpu.VMEM((1, table.shape[1]), jnp.int32),
             pltpu.SMEM((1, table.shape[1]), jnp.int32),
-        ] + [pltpu.VMEM((2 * entries,) + page, BF16)] * d.layers + [pltpu.VMEM((d.slots,) + page, BF16)] * (2 * d.layers) + d.compute_scratch(10, 8) + [
+            pltpu.VMEM((d.tokens, d.width), BF16),
+            pltpu.VMEM((d.tokens, d.width), F32),
+            pltpu.VMEM((d.tokens, d.width), F32),
+            pltpu.VMEM((d.width, HALF), BF16),
+            pltpu.VMEM((HALF, d.width), BF16),
+        ] + [pltpu.VMEM((2 * entries,) + page, BF16)] * d.layers + [pltpu.VMEM((d.slots,) + page, BF16)] * (2 * d.layers) + d.compute_scratch(8, 6) + [
             DMA((4,)),
             DMA((d.layers, 2)),
             DMA,
-            DMA((2,)),
-            DMA((2,)),
-            DMA((d.layers, 2, 2)),
-            DMA((d.layers, 2, 2)),
-            DMA((d.layers, 2, d.kv_heads, 2)),
-            DMA((d.layers, 2, d.kv_heads, 2)),
-            DMA((d.layers, 10, 4)),
-            DMA((d.layers, 10, 4)),
-            DMA,
-        ],
+        ] + [DMA(shape) for shape in ((2,), (d.layers, 2, 2), (d.layers, 2, d.kv_heads, 2), (d.layers, 10, 4)) for _ in PAIR] + [DMA] + [DMA((2,))] * 3,
         compiler_params=pltpu.CompilerParams(collective_id=1, has_side_effects=True, skip_device_barrier=True, vmem_limit_bytes=LIMIT),
         cost_estimate=d.cost(d.layers),
         name="decode_adjacent",
@@ -696,51 +809,38 @@
         at = pl.ds(part * size, size)
         return [pltpu.make_async_copy(*((buf.at[at], dst.at[at]) if out else (src.at[at], buf.at[at])), sem.at[p, part]) for p, (src, buf, dst) in enumerate(pools)]
 
-    def start(copies):
-        for copy in copies:
-            copy.start()
-
-    def wait(copies):
-        for copy in copies:
-            copy.wait()
-
-    def within(ids, count, part, run):
-        @pl.loop(0, count)
-        def _(i):
-            slot = ids(i) - me * d.slots
-            here = (slot >= part * size) & (slot < part * size + size)
-            slot = jnp.clip(slot, 0, d.slots - 1)
-            pl.when(here)(lambda: run(i, slot))
-
-    def row_copies(i, slot):
-        return [pltpu.make_async_copy(last_hbm.at[:, p, i], buf.at[slot], put_sem) for p, (_, buf, _) in enumerate(pools)]
-
-    def clear(i, slot):
-        for _, buf, _ in pools:
-            buf[slot] = jnp.zeros(buf.shape[1:], buf.dtype)
-
-    def last_id(i):
-        return table_s[1, home * d.rows + i]
-
-    @pl.loop(0, parts)
-    def _(part):
-        start(moves(part, False))
-
-    @pl.loop(0, parts)
-    def _(part):
-        wait(moves(part, False))
-        within(last_id, d.rows, part, lambda i, slot: start(row_copies(i, slot)))
-        within(lambda e: src_s[e], src_s.shape[0], part, clear)
-        within(last_id, d.rows, part, lambda i, slot: wait(row_copies(i, slot)))
-        start(moves(part, True))
-
-    @pl.loop(0, parts)
-    def _(part):
-        wait(moves(part, True))
+    def all_parts(out, run):
+        @pl.loop(0, parts)
+        def _(part):
+            for copy in moves(part, out):
+                run(copy)
+
+    start, wait = lambda copy: copy.start(), lambda copy: copy.wait()
+    all_parts(False, start)
+    all_parts(False, wait)
+
+    @pl.loop(0, d.rows)
+    def _(i):
+        slot = local_slot(table_s[1, home * d.rows + i], me, d.slots)
+        for p, (_, buf, _) in enumerate(pools):
+            pltpu.make_async_copy(last_hbm.at[:, p, i], buf.at[slot], put_sem).start()
+
+    @pl.loop(0, src_s.shape[0])
+    def _(e):
+        slot = src_s[e] - me * d.slots
+
+        @pl.when((slot >= 0) & (slot < d.slots))
+        def _():
+            for _, buf, _ in pools:
+                buf[local_slot(src_s[e], me, d.slots)] = jnp.zeros(buf.shape[1:], buf.dtype)
+
+    for src, buf, _ in pools:
+        pltpu.make_async_copy(src.at[pl.ds(0, d.rows)], buf.at[pl.ds(0, d.rows)], put_sem).wait()
+    all_parts(True, start)
+    all_parts(True, wait)
 
 
 def fill_pools(group_size, d, info, table, mig_src, k_pool, v_pool, last):
-    size = 4 * k_pool.size
     return pl.pallas_call(
         functools.partial(fill_pools_kernel, d, group_size),
         out_shape=[jax.ShapeDtypeStruct(k_pool.shape, k_pool.dtype)] * 2,
@@ -748,7 +848,7 @@
         out_specs=[ANY, ANY],
         scratch_shapes=[pltpu.VMEM(k_pool.shape, k_pool.dtype), pltpu.VMEM(k_pool.shape, k_pool.dtype), DMA((2, 4)), DMA],
         compiler_params=pltpu.CompilerParams(vmem_limit_bytes=LIMIT),
-        cost_estimate=pl.CostEstimate(flops=40 * size, bytes_accessed=2 * size, transcendentals=0),
+        cost_estimate=d.cost(1),
         name="fill_pools",
     )(info, table, mig_src, k_pool, v_pool, last)
 
@@ -796,7 +896,7 @@
 def share_kernel(side, k_hbm, v_hbm, k_out, v_out, work, core_buf, ring_buf, load_sem, send_sem, recv_sem, result):
     entries = k_hbm.shape[0]
     exchange = Exchange(side, 0, work, core_buf, ring_buf, result, send_sem, recv_sem)
-    units = [pl.ds(p * entries, entries) for p in range(2)]
+    units = [pl.ds(p * entries, entries) for p in PAIR]
     for p, src in enumerate((k_hbm, v_hbm)):
         pltpu.make_async_copy(src, work.at[0].at[units[p]], load_sem.at[p]).start()
     for p, src in enumerate((k_hbm, v_hbm)):
@@ -973,7 +1073,7 @@
             return lax.dynamic_slice(vec, (dev * rows,), (rows,))
 
         def inside(ids):
-            return jnp.clip(ids - me * slots, 0, slots - 1)
+            return local_slot(ids, me, slots)
 
         def general_path():
             first_new, last_new = new_table[:, 0], new_table[:, 1]

time: 162 us -> 157 us (0.969); the launches traced: 163 us -> 156 us
  Pallas kernels: 151 us -> 147 us
  starting transfers between devices: 5.58 us -> 2.57 us
    ppermute x2, starting transfers between devices: 5.58 us -> 2.57 us  [permute(): lax.ppermute(a, 'kv', perm)]
    pallas_call x1, Pallas kernels: 15.4 us -> 12.5 us  [fill_pools(): pl.pallas_call(functools.partial(fill_pools_kernel, d, group_size), out_s...]
  transfers between devices with their start and end apart: 2 -> 2, of which waited for: 0 -> 1; matrix products, arithmetic and copies ran while one was open for 0% -> 0% of each run, Pallas kernels for 9% -> 8%
where the time goes in v1:
time: 157 us; the launch traced here: 156 us
  Pallas kernels  147 us (94%)
  starting transfers between devices  2.57 us (2%)
  local copies, waits for them, and re-layouts  2.1 us (1%)
    pallas_call x1, Pallas kernels, decode_adjacent(): pl.pallas_call(functools.partial(adjacent_kernel, d, side, group_size, en...  135 us
    pallas_call x1, Pallas kernels, fill_pools(): pl.pallas_call(functools.partial(fill_pools_kernel, d, group_size), out_s...  12.5 us
  transfers between devices with their start and end apart: 2, of which 1 were waited for; matrix products, arithmetic and copies ran while one was open for 0% of the time, Pallas kernels for 8%

profile of v1, /device:TPU:97, one launch (start us, length us, event | category | flops | bytes accessed | tf_op | source)
XLA Modules:
  0.0 155.9 jit_solution(4487143478066639809)
XLA Ops:
  0.6 0.0 copy-start.39
  0.6 134.7 %decode_adjacent.1 = (bf16[2,32,2048]{2,1,0:T(8,128)(2,1)S(1)}, bf16[2,32,2048]{2,1,0:T(8,128)(2,1)S(1)}, s32[2]{0:T(128)S(1)}, bf16[2,2,64,64,128]{4,3,2,1,0:T(8,128)(2,1)}) custom-call(s32[64]{0:T(128)} %src_s.1, s32[64]{0:T(128)} %dst_s.1, s32[2,2048]{1,0:T(2,128)} %bitcast.10.table_hbm, s32[2048]{0:T(1024)} %lens_hbm.1, bf16[16,8,2048]{2,1,0:T(8,128)(2,1)} %bitcast.122, ...), custom_call_target="tpu_custom_call" | custom-call | flops 27917287424 | bytes 218103808 | tf_op jit(solution)/shard_map/decode_adjacent/pallas_call | solution.py:763
  135.4 0.6 fusion.19
  136.6 0.0 copy-done.39
  136.6 0.0 copy-start.37
  136.7 17.4 %conditional.1 = (bf16[2,64,2048]{2,1,0:T(8,128)(2,1)S(1)}, bf16[192,2,64,128]{3,2,1,0:T(8,128)(2,1)}, bf16[192,2,64,128]{3,2,1,0:T(8,128)(2,1)}) conditional(s32[]{:T(128)} %bitcast.15, (bf16[2,32,2048]{2,1,0:T(8,128)(2,1)S(1)}, bf16[2,32,2048]{2,1,0:T(8,128)(2,1)S(1)}, s32[2]{0:T(128)S(1)}, s32[2,2048]{1,0:T(2,128)}, ...), branch_computations={%region_0.0_spmd, %region_1.0_spmd, %region_2.0_spmd, %region_3.0_... | conditional | flops 13959692288 | bytes 114294952 | solution.py:1042
  136.9 2.1 %collective-permute-start.54 = (bf16[2,32,2048]{2,1,0:T(8,128)(2,1)S(1)}, bf16[2,32,2048]{2,1,0:T(8,128)(2,1)S(1)}, u32[]{:S(2)}, u32[]{:S(2)}) collective-permute-start(bf16[2,32,2048]{2,1,0:T(8,128)(2,1)S(1)} %get-tuple-element.1603), channel_id=1, source_target_pairs={{0,5},{1,6},{2,7},{3,8},{4,9},{5,10},{6,11},{7,12},{8,13},{9,14},{... | collective-permute-start | bytes 786440 | tf_op jit(solution)/shard_map/cond/branch_27_fun/ppermute | solution.py:1031
  139.0 0.5 collective-permute-start.55
  139.5 12.5 %fill_pools.59 = (bf16[192,2,64,128]{3,2,1,0:T(8,128)(2,1)}, bf16[192,2,64,128]{3,2,1,0:T(8,128)(2,1)}) custom-call(s32[2]{0:T(128)S(1)} %get-tuple-element.1605.info_s, s32[2,2048]{1,0:T(2,128)} %get-tuple-element.1606.table_s, s32[64]{0:T(128)S(1)} %get-tuple-element.1607.src_s, bf16[192,2,64,128]{3,2,1,0:T(8,128)(2,1)} %get-tuple-element.1608.k_hbm, ...), custom_call_target="tpu_custom_call" | custom-call | flops 13958643712 | bytes 109051904 | tf_op jit(solution)/shard_map/cond/branch_27_fun/fill_pools/pallas_call | solution.py:844
  152.0 0.0 collective-permute-done.54
  152.0 0.0 copy-start.30
  152.1 0.7 copy-done.30
  152.8 0.2 collective-permute-done.55
  153.0 1.1 pad_maximum_fusion.27
  154.0 0.0 copy-start
  154.1 0.8 copy-done
  154.8 0.0 copy-done.37
  154.8 0.9 while.201
Async XLA Ops:
  0.6 136.0 %copy-start.39 = (s32[64]{0:T(128)S(1)}, s32[64]{0:T(128)}, u32[]{:S(2)}) copy-start(s32[64]{0:T(128)} %src_s.1) | copy-start | bytes 772
  136.6 18.2 %copy-start.37 = (s32[64]{0:T(128)S(1)}, s32[64]{0:T(128)}, u32[]{:S(2)}) copy-start(s32[64]{0:T(128)} %dst_s.1) | copy-start | bytes 772
  136.9 15.1 %collective-permute-start.54 = (bf16[2,32,2048]{2,1,0:T(8,128)(2,1)S(1)}, bf16[2,32,2048]{2,1,0:T(8,128)(2,1)S(1)}, u32[]{:S(2)}, u32[]{:S(2)}) collective-permute-start(bf16[2,32,2048]{2,1,0:T(8,128)(2,1)S(1)} %get-tuple-element.1603), channel_id=1, source_target_pairs={{0,5},{1,6},{2,7},{3,8},{4,9},{5,10},{6,11},{7,12},{8,13},{9,14},{... | collective-permute-start | bytes 786440 | tf_op jit(solution)/shard_map/cond/branch_27_fun/ppermute | solution.py:1031
  139.0 13.9 %collective-permute-start.55 = (bf16[2,32,2048]{2,1,0:T(8,128)(2,1)S(1)}, bf16[2,32,2048]{2,1,0:T(8,128)(2,1)}, u32[]{:S(2)}, u32[]{:S(2)}) collective-permute-start(bf16[2,32,2048]{2,1,0:T(8,128)(2,1)S(1)} %get-tuple-element.1604), channel_id=1, source_target_pairs={{0,6},{1,7},{2,8},{3,9},{4,10},{5,11},{6,12},{7,13},{8,14},{9,15},... | collective-permute-start | bytes 786440 | tf_op jit(solution)/shard_map/cond/branch_27_fun/ppermute | solution.py:1031
  152.0 0.7 copy-start.30
  154.0 0.8 copy-start

commit v2 on v1

--- a/solution.py
+++ b/solution.py
@@ -49,7 +49,6 @@
         self.tokens = 2 * rows
         self.stride = self.tokens + 8
         self.n_q, self.n_o, self.n_u = self.q_width // CHUNK, self.width // CHUNK, self.ff // CHUNK
-        self.col_layer = self.n_q + 2 + self.n_o + self.n_u
 
     def compute_scratch(self, n_col, n_row):
         return [
@@ -79,9 +78,9 @@
         self.n_col, self.n_row = self.col_buf.shape[0], self.row_buf.shape[0]
         self.zero = lax.axis_index('kv') * 0
         d = dims
-        self.whole, self.begin = d.ff // 2 // CHUNK, lax.axis_index('kv') % 2 * (d.ff // 2)
-        self.cols = layers * d.col_layer - shared * (d.n_u - self.whole)
-        self.downs = layers * d.n_u - shared * (d.n_u - self.whole)
+        self.whole = d.ff // 2 // CHUNK if shared else d.n_u
+        self.begin = lax.axis_index('kv') % 2 * (d.ff // 2) if shared else 0
+        self.col_layer = d.n_q + 2 + d.n_o + self.whole
         cols = 2 * d.page * d.kv_heads
         col_pos = iota((2 * d.heads, cols), 1)
         row_pos = iota((2 * d.heads, cols), 0)
@@ -97,10 +96,10 @@
         d = self.d
         wq, wk, wv, wo, wu, _ = self.weights
 
-        @pl.when(g < self.cols)
+        @pl.when(g < self.layers * self.col_layer)
         def _():
-            layer = self.layer_of(g, d.col_layer)
-            pos = g - layer * d.col_layer
+            layer = self.layer_of(g, self.col_layer)
+            pos = g - layer * self.col_layer
             slot = g % self.n_col
 
             def go(src, c, begin=0):
@@ -125,17 +124,17 @@
 
             @pl.when(pos >= d.n_q + 2 + d.n_o)
             def _():
-                go(wu, pos - (d.n_q + 2 + d.n_o), self.begin * (layer == self.layers - 1) if self.shared else 0)
+                go(wu, pos - (d.n_q + 2 + d.n_o), self.begin)
 
     def row_start(self, g):
         d = self.d
         wd = self.weights[5]
 
-        @pl.when(g < self.downs)
+        @pl.when(g < self.layers * self.whole)
         def _():
-            layer = self.layer_of(g, d.n_u)
+            layer = self.layer_of(g, self.whole)
             slot = g % self.n_row
-            start = aligned((g - layer * d.n_u) * CHUNK + (self.begin * (layer == self.layers - 1) if self.shared else 0), LANES)
+            start = aligned((g - layer * self.whole) * CHUNK + self.begin, LANES)
             pltpu.make_async_copy(wd.at[self.first + layer].at[pl.ds(start, CHUNK)], self.row_buf.at[slot], self.row_sem.at[slot]).start()
 
     def start_stream(self):
@@ -165,7 +164,7 @@
 
     def project(self, layer):
         d = self.d
-        col0 = (self.zero + layer) * d.col_layer
+        col0 = (self.zero + layer) * self.col_layer
 
         def product(ref):
             return dot(self.y_ref[...], ref[...]).astype(BF16).astype(F32)
@@ -258,14 +257,14 @@
                     at = self.span(many * j + u)
                     self.y_ref[:, at] = (self.y_ref[:, at].astype(F32) + outs[u]).astype(BF16)
 
-            self.with_cols(layer * d.col_layer + d.n_q + len(PAIR) + many * j, many, body)
+            self.with_cols(layer * self.col_layer + d.n_q + len(PAIR) + many * j, many, body)
             if after:
                 after(j)
 
     def mix(self, layer, events=()):
         d = self.d
         layer = self.zero + layer
-        col0 = layer * d.col_layer + d.n_q + 2
+        col0 = layer * self.col_layer + d.n_q + 2
         many = self.group
         pairs = d.n_u // many
 
@@ -291,7 +290,7 @@
                     out += dot(self.act[:, self.span(first + u)], refs[u][...])
                 self.acc[...] = out
 
-            self.with_rows(layer * d.n_u + first, count, body)
+            self.with_rows(layer * self.whole + first, count, body)
 
         @pl.loop(0, pairs)
         def _(j):
@@ -314,18 +313,25 @@
         self.y_ref[...] = self.acc[...].astype(BF16)
 
 
-    def half_start(self):
-        layer, at = self.first + self.layers - 1, pl.ds(aligned(self.begin + self.whole * CHUNK, LANES), HALF)
+    def half_loads(self, layer):
+        at = pl.ds(aligned(self.begin + self.whole * CHUNK, LANES), HALF)
         return (pltpu.make_async_copy(self.weights[4].at[layer].at[:, at], self.half_col, self.half_sem.at[0]),
                 pltpu.make_async_copy(self.weights[5].at[layer].at[at], self.half_row, self.half_sem.at[1]))
 
     def mix_shared(self, layer, send_hidden, wait_hidden, swap_sums, events=()):
         d = self.d
+        half_loads, next_loads = self.half_loads(layer), self.half_loads(layer + 1) if layer + 1 < d.layers else ()
         layer = self.zero + layer
-        col0 = layer * d.col_layer + d.n_q + 2
+        col0 = layer * self.col_layer + d.n_q + 2
         many = self.group
         rows = d.tokens
         offset = d.ff // 2
+        pairs = self.whole // many
+
+        def between(j, first):
+            for k, run in events:
+                if first <= k < first + pairs:
+                    pl.when(j == k - first)(run)
 
         self.out_project(layer, send_hidden)
 
@@ -341,10 +347,9 @@
             self.act[:, pl.ds(aligned(at, LANES), size)] = val[:rows]
             self.act[:, pl.ds(aligned(at + offset, LANES), size)] = val[rows:]
 
-        @pl.loop(0, self.whole // many)
+        @pl.loop(0, pairs)
         def _(j):
-            for k, run in events:
-                pl.when(j == k)(run)
+            between(j, 0)
 
             def body(refs):
                 ups = [dot(hidden(), ref[...]) for ref in refs]
@@ -359,7 +364,7 @@
                 activate(dot(hidden(), refs[0][...]), at, CHUNK)
 
             self.with_cols(col0 + d.n_o + self.whole - tail + u, 1, body)
-        for copy in self.half_start():
+        for copy in half_loads:
             copy.wait()
         activate(dot(hidden(), self.half_col[...]), self.whole * CHUNK, HALF)
 
@@ -370,19 +375,23 @@
             self.acc[...] += out[:rows]
             self.acc_other[...] += out[rows:]
 
-        @pl.loop(0, self.whole // many)
+        @pl.loop(0, pairs)
         def _(j):
+            between(j, pairs)
+
             def body(refs):
                 add(sum(dot(acts((many * j + u) * CHUNK, CHUNK), refs[u][...]) for u in range(many)))
 
-            self.with_rows(layer * d.n_u + many * j, many, body)
+            self.with_rows(layer * self.whole + many * j, many, body)
 
         for u in range(tail):
             def body(refs, at=(self.whole - tail + u) * CHUNK):
                 add(dot(acts(at, CHUNK), refs[0][...]))
 
-            self.with_rows(layer * d.n_u + self.whole - tail + u, 1, body)
+            self.with_rows(layer * self.whole + self.whole - tail + u, 1, body)
         add(dot(acts(self.whole * CHUNK, HALF), self.half_row[...]))
+        for copy in next_loads:
+            copy.start()
         self.y_ref[...] = (self.acc[...] + swap_sums()).astype(BF16)
 
 
@@ -553,7 +562,7 @@
         for load in pool_loads[l]:
             load.start()
     scope("start_stream", dec.start_stream)
-    for copy in dec.half_start():
+    for copy in dec.half_loads(0):
         copy.start()
     shift = scope("load_tables", load_tables)
     home_a = lax.rem(me - shift + group_size, group_size)
@@ -679,6 +688,7 @@
     step_1()
     step_0()
     plan_copy.wait()
+    step_1()
     step_0()
     scope("pages_wait_0", pages_wait, 0)
 
@@ -711,15 +721,6 @@
     def event(run):
         return lambda: run()
 
-    blocks = half // min(UNROLL, half)
-    pairs = 2 * (d.n_u // 2)
-    with jax.named_scope("attend_0"):
-        attend(0, [(0, event(step_1))], [(0, event(step_1))])
-    events = [((2 * k + 1) * pairs // (4 * parts), event(pages_1)) for k in range(2 * parts)]
-    events += [(k * (pairs - 1) // 7, event(step_1)) for k in range(Exchange.STEPS - 4)]
-    events += [(pairs - 1, functools.partial(scope, "finish_0", finish_pages, 0))]
-    with jax.named_scope("mix_0"):
-        dec.mix(0, sorted(events, key=lambda event: event[0]))
     def hidden_copy(at):
         return pltpu.make_async_remote_copy(y_ref.at[:, at], y_other.at[:, at], pair_send.at[0], pair_recv.at[0], device_id={'kv': exchanges[0].partner})
 
@@ -735,18 +736,23 @@
         copy.wait()
         return sums_in[...]
 
-    for l in range(1, d.layers):
-        scope(f"project_{l}", project, l)
-        scope(f"pages_wait_{l}", pages_wait, l)
-        last_wait(l - 1)
+    blocks = half // min(UNROLL, half)
+    last_pair = 2 * (dec.whole // dec.group) - 1
+    for l in range(d.layers):
+        between_a, between_b, events = (), (), []
+        if l:
+            scope(f"project_{l}", project, l)
+            scope(f"pages_wait_{l}", pages_wait, l)
+            last_wait(l - 1)
+        else:
+            between_a, between_b = [(0, event(step_1)), (blocks // 2, event(pages_1))], [(blocks // 2, event(pages_1))]
+            events = [(k * last_pair // 7, event(pages_1)) for k in range(2 * parts - 2)]
+            events += [(k * last_pair // 6, event(step_1)) for k in range(Exchange.STEPS - 4)]
         with jax.named_scope(f"attend_{l}"):
-            attend(l, [], [])
-        finish = [(1, functools.partial(finish_pages, l))]
+            attend(l, between_a, between_b)
+        events += [(last_pair, functools.partial(scope, f"finish_{l}", finish_pages, l))]
         with jax.named_scope(f"mix_{l}"):
-            if l == d.layers - 1:
-                dec.mix_shared(l, send_hidden, wait_hidden, swap_sums, finish)
-            else:
-                dec.mix(l, finish)
+            dec.mix_shared(l, send_hidden, wait_hidden, swap_sums, sorted(events, key=lambda event: event[0]))
     for t in PAIR:
         ya_ref[t] = y_ref[pl.ds(t * d.rows, half), :]
         yb_ref[t] = y_ref[pl.ds(t * d.rows + half, half), :]
@@ -797,47 +803,57 @@
     )(mig_src, mig_dst, table, seq_lens, embeds.reshape(groups, 8, d.width), *weights, k_pool, v_pool)
 
 
-def fill_pools_kernel(dims, group_size, info_s, table_s, src_s, k_hbm, v_hbm, last_hbm, k_out, v_out, k_buf, v_buf, sem, put_sem):
+def fill_pools_kernel(dims, group_size, info_s, table_s, src_s, k_hbm, v_hbm, last_hbm, k_out, v_out, k_buf, v_buf, last, zero, sem, last_sem, put_sem):
     d = dims
     me = lax.axis_index('kv')
     home = lax.rem(me - info_s[0] + group_size, group_size)
     pools = ((k_hbm, k_buf, k_out), (v_hbm, v_buf, v_out))
     parts = sem.shape[1]
     size = d.slots // parts
+    last_load = pltpu.make_async_copy(last_hbm, last, last_sem)
 
     def moves(part, out):
         at = pl.ds(part * size, size)
         return [pltpu.make_async_copy(*((buf.at[at], dst.at[at]) if out else (src.at[at], buf.at[at])), sem.at[p, part]) for p, (src, buf, dst) in enumerate(pools)]
 
-    def all_parts(out, run):
-        @pl.loop(0, parts)
-        def _(part):
-            for copy in moves(part, out):
-                run(copy)
-
-    start, wait = lambda copy: copy.start(), lambda copy: copy.wait()
-    all_parts(False, start)
-    all_parts(False, wait)
-
-    @pl.loop(0, d.rows)
-    def _(i):
-        slot = local_slot(table_s[1, home * d.rows + i], me, d.slots)
-        for p, (_, buf, _) in enumerate(pools):
-            pltpu.make_async_copy(last_hbm.at[:, p, i], buf.at[slot], put_sem).start()
-
-    @pl.loop(0, src_s.shape[0])
-    def _(e):
-        slot = src_s[e] - me * d.slots
-
-        @pl.when((slot >= 0) & (slot < d.slots))
-        def _():
-            for _, buf, _ in pools:
-                buf[local_slot(src_s[e], me, d.slots)] = jnp.zeros(buf.shape[1:], buf.dtype)
-
-    for src, buf, _ in pools:
-        pltpu.make_async_copy(src.at[pl.ds(0, d.rows)], buf.at[pl.ds(0, d.rows)], put_sem).wait()
-    all_parts(True, start)
-    all_parts(True, wait)
+    def all_parts(run):
+        pl.loop(0, parts)(run)
+
+    def start(copies):
+        for copy in copies:
+            copy.start()
+
+    def wait(copies):
+        for copy in copies:
+            copy.wait()
+
+    def puts(run):
+        @pl.loop(0, d.rows)
+        def _(i):
+            slot = local_slot(table_s[1, home * d.rows + i], me, d.slots)
+            run([pltpu.make_async_copy(last.at[:, p, i], dst.at[slot], put_sem) for p, (_, _, dst) in enumerate(pools)])
+
+        @pl.loop(0, src_s.shape[0])
+        def _(e):
+            slot = src_s[e] - me * d.slots
+
+            @pl.when((slot >= 0) & (slot < d.slots))
+            def _():
+                run([pltpu.make_async_copy(zero, dst.at[local_slot(src_s[e], me, d.slots)], put_sem) for _, _, dst in pools])
+
+    all_parts(lambda part: start(moves(part, False)))
+    last_load.start()
+    zero[...] = jnp.zeros_like(zero)
+
+    @all_parts
+    def _(part):
+        wait(moves(part, False))
+        start(moves(part, True))
+
+    last_load.wait()
+    all_parts(lambda part: wait(moves(part, True)))
+    puts(start)
+    puts(wait)
 
 
 def fill_pools(group_size, d, info, table, mig_src, k_pool, v_pool, last):
@@ -846,7 +862,7 @@
         out_shape=[jax.ShapeDtypeStruct(k_pool.shape, k_pool.dtype)] * 2,
         in_specs=[SMEM] * 3 + [ANY] * 3,
         out_specs=[ANY, ANY],
-        scratch_shapes=[pltpu.VMEM(k_pool.shape, k_pool.dtype), pltpu.VMEM(k_pool.shape, k_pool.dtype), DMA((2, 4)), DMA],
+        scratch_shapes=[pltpu.VMEM(shape, BF16) for shape in (k_pool.shape, k_pool.shape, last.shape, k_pool.shape[1:])] + [DMA((2, 4)), DMA, DMA],
         compiler_params=pltpu.CompilerParams(vmem_limit_bytes=LIMIT),
         cost_estimate=d.cost(1),
         name="fill_pools",

time: 157 us -> 159 us (1.013)
  Pallas kernels: 147 us -> 149 us
  transfers between devices with their start and end apart: 2 -> 2, of which waited for: 1 -> 0; matrix products, arithmetic and copies ran while one was open for 0% -> 0% of each run, Pallas kernels for 8% -> 9%
where the time goes in v2:
time: 159 us
  Pallas kernels  149 us (94%)
  starting transfers between devices  4.12 us (3%)
  local copies, waits for them, and re-layouts  2.1 us (1%)
    pallas_call x1, Pallas kernels, decode_adjacent(): pl.pallas_call(functools.partial(adjacent_kernel, d, side, group_size, en...  135 us
    pallas_call x1, Pallas kernels, fill_pools(): pl.pallas_call(functools.partial(fill_pools_kernel, d, group_size), out_s...  14.1 us
    ppermute x2, starting transfers between devices, permute(): lax.ppermute(a, 'kv', perm)  4.12 us
  transfers between devices with their start and end apart: 2, of which 0 were waited for; matrix products, arithmetic and copies ran while one was open for 0% of the time, Pallas kernels for 9%

profile of v2, /device:TPU:97, one launch (start us, length us, event | category | flops | bytes accessed | tf_op | source)
XLA Modules:
  0.0 158.8 jit_solution(8797092401168277938)
XLA Ops:
  0.6 0.0 copy-start.39
  0.6 134.9 %decode_adjacent.1 = (bf16[2,32,2048]{2,1,0:T(8,128)(2,1)S(1)}, bf16[2,32,2048]{2,1,0:T(8,128)(2,1)S(1)}, s32[2]{0:T(128)S(1)}, bf16[2,2,64,64,128]{4,3,2,1,0:T(8,128)(2,1)}) custom-call(s32[64]{0:T(128)} %src_s.1, s32[64]{0:T(128)} %dst_s.1, s32[2,2048]{1,0:T(2,128)} %bitcast.10.table_hbm, s32[2048]{0:T(1024)} %lens_hbm.1, bf16[16,8,2048]{2,1,0:T(8,128)(2,1)} %bitcast.122, ...), custom_call_target="tpu_custom_call" | custom-call | flops 27917287424 | bytes 218103808 | tf_op jit(solution)/shard_map/decode_adjacent/pallas_call | solution.py:769
  135.6 0.6 fusion.19
  136.8 0.0 copy-done.39
  136.8 0.0 copy-start.37
  136.9 20.3 %conditional.1 = (bf16[2,64,2048]{2,1,0:T(8,128)(2,1)S(1)}, bf16[192,2,64,128]{3,2,1,0:T(8,128)(2,1)}, bf16[192,2,64,128]{3,2,1,0:T(8,128)(2,1)}) conditional(s32[]{:T(128)} %bitcast.15, (bf16[2,32,2048]{2,1,0:T(8,128)(2,1)S(1)}, bf16[2,32,2048]{2,1,0:T(8,128)(2,1)S(1)}, s32[2]{0:T(128)S(1)}, s32[2,2048]{1,0:T(2,128)}, ...), branch_computations={%region_0.0_spmd, %region_1.0_spmd, %region_2.0_spmd, %region_3.0_... | conditional | flops 13959692288 | bytes 114294952 | solution.py:1058
  136.9 3.7 %collective-permute-start.2 = (bf16[2,32,2048]{2,1,0:T(8,128)(2,1)S(1)}, bf16[2,32,2048]{2,1,0:T(8,128)(2,1)S(1)}, u32[]{:S(2)}, u32[]{:S(2)}) collective-permute-start(bf16[2,32,2048]{2,1,0:T(8,128)(2,1)S(1)} %get-tuple-element.1353), channel_id=1, source_target_pairs={{0,30},{1,31},{2,0},{3,1},{4,2},{5,3},{6,4},{7,5},{8,6},{9,7},{10,... | collective-permute-start | bytes 786440 | tf_op jit(solution)/shard_map/cond/branch_2_fun/ppermute | solution.py:1047
  140.6 0.5 collective-permute-start.3
  141.0 14.1 %fill_pools.34 = (bf16[192,2,64,128]{3,2,1,0:T(8,128)(2,1)}, bf16[192,2,64,128]{3,2,1,0:T(8,128)(2,1)}) custom-call(s32[2]{0:T(128)S(1)} %get-tuple-element.1355.info_s, s32[2,2048]{1,0:T(2,128)} %get-tuple-element.1356.table_s, s32[64]{0:T(128)S(1)} %get-tuple-element.1357.src_s, bf16[192,2,64,128]{3,2,1,0:T(8,128)(2,1)} %get-tuple-element.1358.k_hbm, ...), custom_call_target="tpu_custom_call" | custom-call | flops 13958643712 | bytes 109051904 | tf_op jit(solution)/shard_map/cond/branch_2_fun/fill_pools/pallas_call | solution.py:860
  155.1 0.0 collective-permute-done.2
  155.1 0.0 copy-start.7
  155.1 0.7 copy-done.7
  155.8 0.0 collective-permute-done.3
  155.8 1.1 pad_maximum_fusion.2
  157.2 0.0 copy-start
  157.2 0.8 copy-done
  158.0 0.0 copy-done.37
  158.0 0.6 while.201
Async XLA Ops:
  0.6 136.2 %copy-start.39 = (s32[64]{0:T(128)S(1)}, s32[64]{0:T(128)}, u32[]{:S(2)}) copy-start(s32[64]{0:T(128)} %src_s.1) | copy-start | bytes 772
  136.8 21.1 %copy-start.37 = (s32[64]{0:T(128)S(1)}, s32[64]{0:T(128)}, u32[]{:S(2)}) copy-start(s32[64]{0:T(128)} %dst_s.1) | copy-start | bytes 772
  136.9 18.2 %collective-permute-start.2 = (bf16[2,32,2048]{2,1,0:T(8,128)(2,1)S(1)}, bf16[2,32,2048]{2,1,0:T(8,128)(2,1)S(1)}, u32[]{:S(2)}, u32[]{:S(2)}) collective-permute-start(bf16[2,32,2048]{2,1,0:T(8,128)(2,1)S(1)} %get-tuple-element.1353), channel_id=1, source_target_pairs={{0,30},{1,31},{2,0},{3,1},{4,2},{5,3},{6,4},{7,5},{8,6},{9,7},{10,... | collective-permute-start | bytes 786440 | tf_op jit(solution)/shard_map/cond/branch_2_fun/ppermute | solution.py:1047
  140.6 15.3 %collective-permute-start.3 = (bf16[2,32,2048]{2,1,0:T(8,128)(2,1)S(1)}, bf16[2,32,2048]{2,1,0:T(8,128)(2,1)}, u32[]{:S(2)}, u32[]{:S(2)}) collective-permute-start(bf16[2,32,2048]{2,1,0:T(8,128)(2,1)S(1)} %get-tuple-element.1354), channel_id=1, source_target_pairs={{0,31},{1,0},{2,1},{3,2},{4,3},{5,4},{6,5},{7,6},{8,7},{9,8},{10,9... | collective-permute-start | bytes 786440 | tf_op jit(solution)/shard_map/cond/branch_2_fun/ppermute | solution.py:1047
  155.1 0.7 copy-start.7
  157.2 0.8 copy-start

commit v3 on v2

--- a/solution.py
+++ b/solution.py
@@ -664,32 +664,31 @@
     scope("plan", plan)
     step_0()
     pages_0()
-    step_0()
-    pages_0()
-    scope("pass_on", pass_on)
-    step_0()
-    pages_0()
     for l in range(1, d.layers):
         for load in pool_loads[l]:
             load.wait()
+    scope("own_1", own, 1)
+
+    def both():
+        step_0()
+        pages_0()
+        step_1()
+
+    both()
+    scope("pass_on", pass_on)
+    both()
+    both()
+    scope("pack_1", pack, 1)
+    both()
+    scope("take_embeddings", take_embeddings)
+    both()
+    scope("project_0", project, 0)
+    both()
+    plan_copy.wait()
     step_0()
-    pages_0()
-    scope("own_1", own, 1)
-    step_0()
-    pages_0()
-    scope("pack_1", pack, 1)
-    step_0()
-    pages_0()
-    scope("take_embeddings", take_embeddings)
     step_1()
     step_0()
-    pages_0()
-    scope("project_0", project, 0)
     step_1()
-    step_0()
-    plan_copy.wait()
-    step_1()
-    step_0()
     scope("pages_wait_0", pages_wait, 0)
 
     def attend(l, events_a, events_b):
@@ -745,9 +744,9 @@
             scope(f"pages_wait_{l}", pages_wait, l)
             last_wait(l - 1)
         else:
-            between_a, between_b = [(0, event(step_1)), (blocks // 2, event(pages_1))], [(blocks // 2, event(pages_1))]
+            between_a, between_b = [(0, event(step_1)), (blocks // 2, event(pages_1))], [(0, event(step_1)), (blocks // 2, event(pages_1))]
             events = [(k * last_pair // 7, event(pages_1)) for k in range(2 * parts - 2)]
-            events += [(k * last_pair // 6, event(step_1)) for k in range(Exchange.STEPS - 4)]
+            events += [(1, event(step_1))]
         with jax.named_scope(f"attend_{l}"):
             attend(l, between_a, between_b)
         events += [(last_pair, functools.partial(scope, f"finish_{l}", finish_pages, l))]
@@ -803,57 +802,47 @@
     )(mig_src, mig_dst, table, seq_lens, embeds.reshape(groups, 8, d.width), *weights, k_pool, v_pool)
 
 
-def fill_pools_kernel(dims, group_size, info_s, table_s, src_s, k_hbm, v_hbm, last_hbm, k_out, v_out, k_buf, v_buf, last, zero, sem, last_sem, put_sem):
+def fill_pools_kernel(dims, group_size, info_s, table_s, src_s, k_hbm, v_hbm, last_hbm, k_out, v_out, k_buf, v_buf, sem, put_sem):
     d = dims
     me = lax.axis_index('kv')
     home = lax.rem(me - info_s[0] + group_size, group_size)
     pools = ((k_hbm, k_buf, k_out), (v_hbm, v_buf, v_out))
     parts = sem.shape[1]
     size = d.slots // parts
-    last_load = pltpu.make_async_copy(last_hbm, last, last_sem)
 
     def moves(part, out):
         at = pl.ds(part * size, size)
         return [pltpu.make_async_copy(*((buf.at[at], dst.at[at]) if out else (src.at[at], buf.at[at])), sem.at[p, part]) for p, (src, buf, dst) in enumerate(pools)]
 
-    def all_parts(run):
-        pl.loop(0, parts)(run)
-
-    def start(copies):
-        for copy in copies:
-            copy.start()
-
-    def wait(copies):
-        for copy in copies:
-            copy.wait()
-
-    def puts(run):
-        @pl.loop(0, d.rows)
-        def _(i):
-            slot = local_slot(table_s[1, home * d.rows + i], me, d.slots)
-            run([pltpu.make_async_copy(last.at[:, p, i], dst.at[slot], put_sem) for p, (_, _, dst) in enumerate(pools)])
-
-        @pl.loop(0, src_s.shape[0])
-        def _(e):
-            slot = src_s[e] - me * d.slots
-
-            @pl.when((slot >= 0) & (slot < d.slots))
-            def _():
-                run([pltpu.make_async_copy(zero, dst.at[local_slot(src_s[e], me, d.slots)], put_sem) for _, _, dst in pools])
-
-    all_parts(lambda part: start(moves(part, False)))
-    last_load.start()
-    zero[...] = jnp.zeros_like(zero)
-
-    @all_parts
-    def _(part):
-        wait(moves(part, False))
-        start(moves(part, True))
-
-    last_load.wait()
-    all_parts(lambda part: wait(moves(part, True)))
-    puts(start)
-    puts(wait)
+    def all_parts(out, run):
+        @pl.loop(0, parts)
+        def _(part):
+            for copy in moves(part, out):
+                run(copy)
+
+    start, wait = lambda copy: copy.start(), lambda copy: copy.wait()
+    all_parts(False, start)
+    all_parts(False, wait)
+
+    @pl.loop(0, d.rows)
+    def _(i):
+        slot = local_slot(table_s[1, home * d.rows + i], me, d.slots)
+        for p, (_, buf, _) in enumerate(pools):
+            pltpu.make_async_copy(last_hbm.at[:, p, i], buf.at[slot], put_sem).start()
+
+    @pl.loop(0, src_s.shape[0])
+    def _(e):
+        slot = src_s[e] - me * d.slots
+
+        @pl.when((slot >= 0) & (slot < d.slots))
+        def _():
+            for _, buf, _ in pools:
+                buf[local_slot(src_s[e], me, d.slots)] = jnp.zeros(buf.shape[1:], buf.dtype)
+
+    for src, buf, _ in pools:
+        pltpu.make_async_copy(src.at[pl.ds(0, d.rows)], buf.at[pl.ds(0, d.rows)], put_sem).wait()
+    all_parts(True, start)
+    all_parts(True, wait)
 
 
 def fill_pools(group_size, d, info, table, mig_src, k_pool, v_pool, last):
@@ -862,7 +851,7 @@
         out_shape=[jax.ShapeDtypeStruct(k_pool.shape, k_pool.dtype)] * 2,
         in_specs=[SMEM] * 3 + [ANY] * 3,
         out_specs=[ANY, ANY],
-        scratch_shapes=[pltpu.VMEM(shape, BF16) for shape in (k_pool.shape, k_pool.shape, last.shape, k_pool.shape[1:])] + [DMA((2, 4)), DMA, DMA],
+        scratch_shapes=[pltpu.VMEM(k_pool.shape, k_pool.dtype), pltpu.VMEM(k_pool.shape, k_pool.dtype), DMA((2, 4)), DMA],
         compiler_params=pltpu.CompilerParams(vmem_limit_bytes=LIMIT),
         cost_estimate=d.cost(1),
         name="fill_pools",

time: 159 us -> 157 us (0.987)
  transfers between devices with their start and end apart: 2 -> 2, of which waited for: 0 -> 1; matrix products, arithmetic and copies ran while one was open for 0% -> 0% of each run, Pallas kernels for 9% -> 8%
where the time goes in v3:
time: 157 us; the launch traced here: 158 us
  Pallas kernels  148 us (94%)
  starting transfers between devices  2.66 us (2%)
  local copies, waits for them, and re-layouts  2.1 us (1%)
    pallas_call x1, Pallas kernels, decode_adjacent(): pl.pallas_call(functools.partial(adjacent_kernel, d, side, group_size, en...  136 us
    pallas_call x1, Pallas kernels, fill_pools(): pl.pallas_call(functools.partial(fill_pools_kernel, d, group_size), out_s...  12.5 us
  transfers between devices with their start and end apart: 2, of which 1 were waited for; matrix products, arithmetic and copies ran while one was open for 0% of the time, Pallas kernels for 8%

profile of v3, /device:TPU:97, one launch (start us, length us, event | category | flops | bytes accessed | tf_op | source)
XLA Modules:
  0.0 158.0 jit_solution(16944771867425067224)
XLA Ops:
  0.6 0.0 copy-start.39
  0.6 135.9 %decode_adjacent.1 = (bf16[2,32,2048]{2,1,0:T(8,128)(2,1)S(1)}, bf16[2,32,2048]{2,1,0:T(8,128)(2,1)S(1)}, s32[2]{0:T(128)S(1)}, bf16[2,2,64,64,128]{4,3,2,1,0:T(8,128)(2,1)}) custom-call(s32[64]{0:T(128)} %src_s.1, s32[64]{0:T(128)} %dst_s.1, s32[2,2048]{1,0:T(2,128)} %bitcast.10.table_hbm, s32[2048]{0:T(1024)} %lens_hbm.1, bf16[16,8,2048]{2,1,0:T(8,128)(2,1)} %bitcast.122, ...), custom_call_target="tpu_custom_call" | custom-call | flops 27917287424 | bytes 218103808 | tf_op jit(solution)/shard_map/decode_adjacent/pallas_call | solution.py:768
  136.5 0.6 fusion.19
  137.8 0.0 copy-done.39
  137.8 0.0 copy-start.37
  137.8 18.5 %conditional.1 = (bf16[2,64,2048]{2,1,0:T(8,128)(2,1)S(1)}, bf16[192,2,64,128]{3,2,1,0:T(8,128)(2,1)}, bf16[192,2,64,128]{3,2,1,0:T(8,128)(2,1)}) conditional(s32[]{:T(128)} %bitcast.15, (bf16[2,32,2048]{2,1,0:T(8,128)(2,1)S(1)}, bf16[2,32,2048]{2,1,0:T(8,128)(2,1)S(1)}, s32[2]{0:T(128)S(1)}, s32[2,2048]{1,0:T(2,128)}, ...), branch_computations={%region_0.0_spmd, %region_1.0_spmd, %region_2.0_spmd, %region_3.0_... | conditional | flops 13959692288 | bytes 114294952 | solution.py:1047
  137.9 0.1 collective-permute-start.38
  138.0 2.5 %collective-permute-start.39 = (bf16[2,32,2048]{2,1,0:T(8,128)(2,1)S(1)}, bf16[2,32,2048]{2,1,0:T(8,128)(2,1)}, u32[]{:S(2)}, u32[]{:S(2)}) collective-permute-start(bf16[2,32,2048]{2,1,0:T(8,128)(2,1)S(1)} %get-tuple-element.1524), channel_id=1, source_target_pairs={{0,14},{1,15},{2,16},{3,17},{4,18},{5,19},{6,20},{7,21},{8,22},{9,... | collective-permute-start | bytes 786440 | tf_op jit(solution)/shard_map/cond/branch_19_fun/ppermute | solution.py:1036
  140.5 12.5 %fill_pools.51 = (bf16[192,2,64,128]{3,2,1,0:T(8,128)(2,1)}, bf16[192,2,64,128]{3,2,1,0:T(8,128)(2,1)}) custom-call(s32[2]{0:T(128)S(1)} %get-tuple-element.1525.info_s, s32[2,2048]{1,0:T(2,128)} %get-tuple-element.1526.table_s, s32[64]{0:T(128)S(1)} %get-tuple-element.1527.src_s, bf16[192,2,64,128]{3,2,1,0:T(8,128)(2,1)} %get-tuple-element.1528.k_hbm, ...), custom_call_target="tpu_custom_call" | custom-call | flops 13958643712 | bytes 109051904 | tf_op jit(solution)/shard_map/cond/branch_19_fun/fill_pools/pallas_call | solution.py:849
  153.1 0.0 collective-permute-done.38
  153.1 0.0 copy-start.22
  153.1 0.7 copy-done.22
  153.8 1.2 collective-permute-done.39
  155.0 1.1 pad_maximum_fusion.19
  156.3 0.0 copy-start
  156.3 0.8 copy-done
  157.1 0.0 copy-done.37
  157.1 0.6 while.201
Async XLA Ops:
  0.6 137.2 %copy-start.39 = (s32[64]{0:T(128)S(1)}, s32[64]{0:T(128)}, u32[]{:S(2)}) copy-start(s32[64]{0:T(128)} %src_s.1) | copy-start | bytes 772
  137.8 19.3 %copy-start.37 = (s32[64]{0:T(128)S(1)}, s32[64]{0:T(128)}, u32[]{:S(2)}) copy-start(s32[64]{0:T(128)} %dst_s.1) | copy-start | bytes 772
  137.9 15.2 %collective-permute-start.38 = (bf16[2,32,2048]{2,1,0:T(8,128)(2,1)S(1)}, bf16[2,32,2048]{2,1,0:T(8,128)(2,1)S(1)}, u32[]{:S(2)}, u32[]{:S(2)}) collective-permute-start(bf16[2,32,2048]{2,1,0:T(8,128)(2,1)S(1)} %get-tuple-element.1523), channel_id=1, source_target_pairs={{0,13},{1,14},{2,15},{3,16},{4,17},{5,18},{6,19},{7,20},{8,21},{9,... | collective-permute-start | bytes 786440 | tf_op jit(solution)/shard_map/cond/branch_19_fun/ppermute | solution.py:1036
  138.0 17.0 %collective-permute-start.39 = (bf16[2,32,2048]{2,1,0:T(8,128)(2,1)S(1)}, bf16[2,32,2048]{2,1,0:T(8,128)(2,1)}, u32[]{:S(2)}, u32[]{:S(2)}) collective-permute-start(bf16[2,32,2048]{2,1,0:T(8,128)(2,1)S(1)} %get-tuple-element.1524), channel_id=1, source_target_pairs={{0,14},{1,15},{2,16},{3,17},{4,18},{5,19},{6,20},{7,21},{8,22},{9,... | collective-permute-start | bytes 786440 | tf_op jit(solution)/shard_map/cond/branch_19_fun/ppermute | solution.py:1036
  153.1 0.7 copy-start.22
  156.3 0.8 copy-start

commit v4 on v3

--- a/solution.py
+++ b/solution.py
@@ -14,10 +14,11 @@
 DMA = pltpu.SemaphoreType.DMA
 CHUNK = 256
 UNROLL = 8
+MLP_GROUP = 3
 LANES = 128
 HALF = CHUNK // 2
 PAIR = (0, 1)
-LIMIT = 63 << 20
+LIMIT = 1023 << 16
 F32, BF16 = jnp.float32, jnp.bfloat16
 
 
@@ -323,7 +324,7 @@
         half_loads, next_loads = self.half_loads(layer), self.half_loads(layer + 1) if layer + 1 < d.layers else ()
         layer = self.zero + layer
         col0 = layer * self.col_layer + d.n_q + 2
-        many = self.group
+        many = MLP_GROUP
         rows = d.tokens
         offset = d.ff // 2
         pairs = self.whole // many
@@ -688,7 +689,6 @@
     step_0()
     step_1()
     step_0()
-    step_1()
     scope("pages_wait_0", pages_wait, 0)
 
     def attend(l, events_a, events_b):
@@ -736,7 +736,7 @@
         return sums_in[...]
 
     blocks = half // min(UNROLL, half)
-    last_pair = 2 * (dec.whole // dec.group) - 1
+    last_pair = 2 * (dec.whole // MLP_GROUP) - 1
     for l in range(d.layers):
         between_a, between_b, events = (), (), []
         if l:
@@ -744,9 +744,9 @@
             scope(f"pages_wait_{l}", pages_wait, l)
             last_wait(l - 1)
         else:
-            between_a, between_b = [(0, event(step_1)), (blocks // 2, event(pages_1))], [(0, event(step_1)), (blocks // 2, event(pages_1))]
+            between_a, between_b = [(blocks // 2, event(step_1))], [(0, event(pages_1)), (blocks // 2, event(pages_1))]
             events = [(k * last_pair // 7, event(pages_1)) for k in range(2 * parts - 2)]
-            events += [(1, event(step_1))]
+            events += [(k * last_pair // 3, event(step_1)) for k in PAIR] + [(last_pair - parts, event(step_1))]
         with jax.named_scope(f"attend_{l}"):
             attend(l, between_a, between_b)
         events += [(last_pair, functools.partial(scope, f"finish_{l}", finish_pages, l))]

time: 157 us -> 152 us (0.968); the launches traced: 158 us -> 155 us
  Pallas kernels: 148 us -> 144 us
  waiting for transfers between devices: 1.25 us -> 5.13 us
  starting transfers between devices: 2.66 us -> 0.38 us
    pallas_call x1, Pallas kernels: 136 us -> 131 us  [decode_adjacent(): pl.pallas_call(functools.partial(adjacent_kernel, d, side, group_size, en...]
    ppermute x2, waiting for transfers between devices: 1.25 us -> 5.13 us  [permute(): lax.ppermute(a, 'kv', perm)]
    ppermute x2, starting transfers between devices: 2.66 us -> 0.38 us  [permute(): lax.ppermute(a, 'kv', perm)]
  transfers between devices with their start and end apart: 2 -> 2, of which waited for: 1 -> 2; matrix products, arithmetic and copies ran while one was open for 0% -> 0% of each run, Pallas kernels for 8% -> 8%
where the time goes in v4:
time: 152 us; the launch traced here: 155 us
  Pallas kernels  144 us (95%)
  waiting for transfers between devices  5.13 us (3%)
  other arithmetic  1.87 us (1%)
    pallas_call x1, Pallas kernels, decode_adjacent(): pl.pallas_call(functools.partial(adjacent_kernel, d, side, group_size, en...  131 us
    pallas_call x1, Pallas kernels, fill_pools(): pl.pallas_call(functools.partial(fill_pools_kernel, d, group_size), out_s...  12.5 us
    ppermute x2, waiting for transfers between devices, permute(): lax.ppermute(a, 'kv', perm)  5.13 us
  transfers between devices with their start and end apart: 2, of which 2 were waited for; matrix products, arithmetic and copies ran while one was open for 0% of the time, Pallas kernels for 8%

profile of v4, /device:TPU:97, one launch (start us, length us, event | category | flops | bytes accessed | tf_op | source)
XLA Modules:
  0.0 154.8 jit_solution(7282051379845932170)
XLA Ops:
  0.6 131.5 %decode_adjacent.1 = (bf16[2,32,2048]{2,1,0:T(8,128)(2,1)}, bf16[2,32,2048]{2,1,0:T(8,128)(2,1)}, s32[2]{0:T(128)}, bf16[2,2,64,64,128]{4,3,2,1,0:T(8,128)(2,1)}) custom-call(s32[64]{0:T(128)} %src_s.1, s32[64]{0:T(128)} %dst_s.1, s32[2,2048]{1,0:T(2,128)} %bitcast.134, s32[2048]{0:T(1024)} %lens_hbm.1, bf16[16,8,2048]{2,1,0:T(8,128)(2,1)} %bitcast.122, ...), custom_call_target="tpu_custom_call" | custom-call | flops 27917287424 | bytes 218103808 | tf_op jit(solution)/shard_map/decode_adjacent/pallas_call | solution.py:768
  132.1 1.3 fusion.19
  134.1 19.9 %conditional.1 = (bf16[2,64,2048]{2,1,0:T(8,128)(2,1)}, bf16[192,2,64,128]{3,2,1,0:T(8,128)(2,1)}, bf16[192,2,64,128]{3,2,1,0:T(8,128)(2,1)}) conditional(s32[]{:T(128)} %bitcast.15, (bf16[2,32,2048]{2,1,0:T(8,128)(2,1)}, bf16[2,32,2048]{2,1,0:T(8,128)(2,1)}, s32[2]{0:T(128)}, s32[2,2048]{1,0:T(2,128)}, s32[64]{0:T(128)}, ...), branch_computations={%region_0.0_spmd, %region_1.0_spmd, %region_2.0_spmd, %region_3.0_... | conditional | flops 13959692288 | bytes 113246352 | solution.py:1047
  134.1 0.1 collective-permute-start.44
  134.2 0.3 collective-permute-start.45
  134.5 12.5 %fill_pools.54 = (bf16[192,2,64,128]{3,2,1,0:T(8,128)(2,1)}, bf16[192,2,64,128]{3,2,1,0:T(8,128)(2,1)}) custom-call(s32[2]{0:T(128)} %get-tuple-element.1555.info_s, s32[2,2048]{1,0:T(2,128)} %get-tuple-element.1556.table_s, s32[64]{0:T(128)} %get-tuple-element.1557.src_s, bf16[192,2,64,128]{3,2,1,0:T(8,128)(2,1)} %get-tuple-element.1558.k_hbm, ...), custom_call_target="tpu_custom_call" | custom-call | flops 13958643712 | bytes 109051904 | tf_op jit(solution)/shard_map/cond/branch_22_fun/fill_pools/pallas_call | solution.py:849
  147.0 0.8 collective-permute-done.44
  147.9 4.3 %collective-permute-done.45 = bf16[2,32,2048]{2,1,0:T(8,128)(2,1)} collective-permute-done((bf16[2,32,2048]{2,1,0:T(8,128)(2,1)}, bf16[2,32,2048]{2,1,0:T(8,128)(2,1)}, u32[]{:S(2)}, u32[]{:S(2)}) %collective-permute-start.45) | collective-permute-done | bytes 262176 | tf_op jit(solution)/shard_map/cond/branch_22_fun/ppermute | solution.py:1036
  152.2 1.9 %pad_maximum_fusion.22 = bf16[2,64,2048]{2,1,0:T(8,128)(2,1)} fusion(bf16[2,32,2048]{2,1,0:T(8,128)(2,1)} %collective-permute-done.45, bf16[2,32,2048]{2,1,0:T(8,128)(2,1)} %collective-permute-done.44), kind=kLoop, calls=%fused_computation.23 | loop fusion | flops 1048576 | bytes 1048576 | tf_op jit(solution)/shard_map/cond/branch_22_fun/concatenate | solution.py:1043
  154.0 0.6 while.201
Async XLA Ops:
  134.1 13.7 %collective-permute-start.44 = (bf16[2,32,2048]{2,1,0:T(8,128)(2,1)}, bf16[2,32,2048]{2,1,0:T(8,128)(2,1)}, u32[]{:S(2)}, u32[]{:S(2)}) collective-permute-start(bf16[2,32,2048]{2,1,0:T(8,128)(2,1)} %get-tuple-element.1553), channel_id=1, source_target_pairs={{0,10},{1,11},{2,12},{3,13},{4,14},{5,15},{6,16},{7,17},{8,18},{9,... | collective-permute-start | bytes 786440 | tf_op jit(solution)/shard_map/cond/branch_22_fun/ppermute | solution.py:1036
  134.2 17.9 %collective-permute-start.45 = (bf16[2,32,2048]{2,1,0:T(8,128)(2,1)}, bf16[2,32,2048]{2,1,0:T(8,128)(2,1)}, u32[]{:S(2)}, u32[]{:S(2)}) collective-permute-start(bf16[2,32,2048]{2,1,0:T(8,128)(2,1)} %get-tuple-element.1554), channel_id=1, source_target_pairs={{0,11},{1,12},{2,13},{3,14},{4,15},{5,16},{6,17},{7,18},{8,19},{9,... | collective-permute-start | bytes 786440 | tf_op jit(solution)/shard_map/cond/branch_22_fun/ppermute | solution.py:1036

commit v5 on v4

--- a/solution.py
+++ b/solution.py
@@ -1030,8 +1030,6 @@
 
 
 def permute(arrays, shift, group_size):
-    if shift == group_size // 2:
-        return permute(permute(arrays, shift // 2, group_size), shift // 2, group_size)
     perm = [(i, (i + shift) % group_size) for i in range(group_size)]
     return jax.tree.map(lambda a: lax.ppermute(a, 'kv', perm), arrays) if shift else arrays
 

time: 152 us -> 152 us (level)
  waiting for transfers between devices: 5.13 us -> 1.93 us
  starting transfers between devices: 0.38 us -> 2.07 us
    ppermute x2, waiting for transfers between devices: 5.13 us -> 1.93 us  [permute(): lax.ppermute(a, 'kv', perm)]
    ppermute x2, starting transfers between devices: 0.38 us -> 2.07 us  [permute(): lax.ppermute(a, 'kv', perm)]
  transfers between devices with their start and end apart: 2 -> 2, of which waited for: 2 -> 1; matrix products, arithmetic and copies ran while one was open for 0% -> 0% of each run, Pallas kernels for 8% -> 8%
where the time goes in v5:
time: 152 us; the launch traced here: 153 us
  Pallas kernels  144 us (95%)
  starting transfers between devices  2.07 us (1%)
  waiting for transfers between devices  1.93 us (1%)
  other arithmetic  1.87 us (1%)
    pallas_call x1, Pallas kernels, decode_adjacent(): pl.pallas_call(functools.partial(adjacent_kernel, d, side, group_size, en...  131 us
    pallas_call x1, Pallas kernels, fill_pools(): pl.pallas_call(functools.partial(fill_pools_kernel, d, group_size), out_s...  12.5 us
  transfers between devices with their start and end apart: 2, of which 1 were waited for; matrix products, arithmetic and copies ran while one was open for 0% of the time, Pallas kernels for 8%

profile of v5, /device:TPU:97, one launch (start us, length us, event | category | flops | bytes accessed | tf_op | source)
XLA Modules:
  0.0 153.3 jit_solution(7484010500224820523)
XLA Ops:
  0.6 131.5 %decode_adjacent.1 = (bf16[2,32,2048]{2,1,0:T(8,128)(2,1)}, bf16[2,32,2048]{2,1,0:T(8,128)(2,1)}, s32[2]{0:T(128)}, bf16[2,2,64,64,128]{4,3,2,1,0:T(8,128)(2,1)}) custom-call(s32[64]{0:T(128)} %src_s.1, s32[64]{0:T(128)} %dst_s.1, s32[2,2048]{1,0:T(2,128)} %bitcast.134, s32[2048]{0:T(1024)} %lens_hbm.1, bf16[16,8,2048]{2,1,0:T(8,128)(2,1)} %bitcast.122, ...), custom_call_target="tpu_custom_call" | custom-call | flops 27917287424 | bytes 218103808 | tf_op jit(solution)/shard_map/decode_adjacent/pallas_call | solution.py:768
  132.1 1.3 fusion.19
  134.1 18.4 %conditional.1 = (bf16[2,64,2048]{2,1,0:T(8,128)(2,1)}, bf16[192,2,64,128]{3,2,1,0:T(8,128)(2,1)}, bf16[192,2,64,128]{3,2,1,0:T(8,128)(2,1)}) conditional(s32[]{:T(128)} %bitcast.15, (bf16[2,32,2048]{2,1,0:T(8,128)(2,1)}, bf16[2,32,2048]{2,1,0:T(8,128)(2,1)}, s32[2]{0:T(128)}, s32[2,2048]{1,0:T(2,128)}, s32[64]{0:T(128)}, ...), branch_computations={%region_0.0_spmd, %region_1.0_spmd, %region_2.0_spmd, %region_3.0_... | conditional | flops 13959692288 | bytes 112197736 | solution.py:1045
  134.1 0.1 collective-permute-start.22
  134.2 2.0 %collective-permute-start.23 = (bf16[2,32,2048]{2,1,0:T(8,128)(2,1)}, bf16[2,32,2048]{2,1,0:T(8,128)(2,1)}, u32[]{:S(2)}, u32[]{:S(2)}) collective-permute-start(bf16[2,32,2048]{2,1,0:T(8,128)(2,1)} %get-tuple-element.1454), channel_id=1, source_target_pairs={{0,21},{1,22},{2,23},{3,24},{4,25},{5,26},{6,27},{7,28},{8,29},{9,... | collective-permute-start | bytes 786440 | tf_op jit(solution)/shard_map/cond/branch_12_fun/ppermute | solution.py:1034
  136.2 12.5 %fill_pools.44 = (bf16[192,2,64,128]{3,2,1,0:T(8,128)(2,1)}, bf16[192,2,64,128]{3,2,1,0:T(8,128)(2,1)}) custom-call(s32[2]{0:T(128)} %get-tuple-element.1455.info_s, s32[2,2048]{1,0:T(2,128)} %get-tuple-element.1456.table_s, s32[64]{0:T(128)} %get-tuple-element.1457.src_s, bf16[192,2,64,128]{3,2,1,0:T(8,128)(2,1)} %get-tuple-element.1458.k_hbm, ...), custom_call_target="tpu_custom_call" | custom-call | flops 13958643712 | bytes 109051904 | tf_op jit(solution)/shard_map/cond/branch_12_fun/fill_pools/pallas_call | solution.py:849
  148.7 0.0 collective-permute-done.22
  148.7 1.9 %collective-permute-done.23 = bf16[2,32,2048]{2,1,0:T(8,128)(2,1)} collective-permute-done((bf16[2,32,2048]{2,1,0:T(8,128)(2,1)}, bf16[2,32,2048]{2,1,0:T(8,128)(2,1)}, u32[]{:S(2)}, u32[]{:S(2)}) %collective-permute-start.23) | collective-permute-done | bytes 262176 | tf_op jit(solution)/shard_map/cond/branch_12_fun/ppermute | solution.py:1034
  150.6 1.9 %pad_maximum_fusion.12 = bf16[2,64,2048]{2,1,0:T(8,128)(2,1)} fusion(bf16[2,32,2048]{2,1,0:T(8,128)(2,1)} %collective-permute-done.23, bf16[2,32,2048]{2,1,0:T(8,128)(2,1)} %collective-permute-done.22), kind=kLoop, calls=%fused_computation.13 | loop fusion | flops 1048576 | bytes 1048576 | tf_op jit(solution)/shard_map/cond/branch_12_fun/concatenate | solution.py:1041
  152.5 0.6 while.201
Async XLA Ops:
  134.1 14.6 %collective-permute-start.22 = (bf16[2,32,2048]{2,1,0:T(8,128)(2,1)}, bf16[2,32,2048]{2,1,0:T(8,128)(2,1)}, u32[]{:S(2)}, u32[]{:S(2)}) collective-permute-start(bf16[2,32,2048]{2,1,0:T(8,128)(2,1)} %get-tuple-element.1453), channel_id=1, source_target_pairs={{0,20},{1,21},{2,22},{3,23},{4,24},{5,25},{6,26},{7,27},{8,28},{9,... | collective-permute-start | bytes 786440 | tf_op jit(solution)/shard_map/cond/branch_12_fun/ppermute | solution.py:1034
  134.2 16.4 %collective-permute-start.23 = (bf16[2,32,2048]{2,1,0:T(8,128)(2,1)}, bf16[2,32,2048]{2,1,0:T(8,128)(2,1)}, u32[]{:S(2)}, u32[]{:S(2)}) collective-permute-start(bf16[2,32,2048]{2,1,0:T(8,128)(2,1)} %get-tuple-element.1454), channel_id=1, source_target_pairs={{0,21},{1,22},{2,23},{3,24},{4,25},{5,26},{6,27},{7,28},{8,29},{9,... | collective-permute-start | bytes 786440 | tf_op jit(solution)/shard_map/cond/branch_12_fun/ppermute | solution.py:1034
